TPU v7x, 32 devices: a 4x4x1 block of a 4x4x8 slice. The times are simulated.
32 devices in a mesh: part: 1 (over z), data: 4 (over y), seq: 8 (over x, core).
Axes of the slice: x: 4, y: 4, z: 1, core: 2. Of those that a mesh axis runs over, the one named last changes fastest.
The devices are a block of a 4x4x8 slice.
Arguments:
- enc_out: bfloat16 [64, 64, 640], P(('part', 'data'), 'seq')
- pred_out: bfloat16 [64, 32, 640], P(('part', 'data'))
- w_enc: bfloat16 [640, 640], replicated
- w_pred: bfloat16 [640, 640], replicated
- w_out: bfloat16 [640, 4096], replicated
- labels: int32 [64, 31], P(('part', 'data'))
- frame_len: int32 [64], P(('part', 'data'))
- label_len: int32 [64], P(('part', 'data'))
Outputs:
- output 1: float32 [64], P(('part', 'data'))
- output 2: bfloat16 [64, 64, 640], P(('part', 'data'), 'seq')
- output 3: float32 [64, 32, 640], P(('part', 'data'))
- output 4: float32 [640, 640], P('part')
- output 5: float32 [640, 640], P('part')
- output 6: float32 [640, 4096], P('part')
All inputs are finite; a program needn't handle non-finite values.
Results may differ from a plain program's by a relative error of at most 0.0125531.
Values are sent between devices in bfloat16 or wider.
A program may use at most 768 MiB of HBM per device.

v0:
```python
import jax
import jax.numpy as jnp
from jax import lax
from jax.sharding import PartitionSpec as P

NEG_FILL = -1e30


def joint_forward(enc_loc, pred_loc, w_enc, w_pred, w_out, lab_ids):
    act_enc = jnp.einsum("bth,hj->btj", enc_loc, w_enc, preferred_element_type=jnp.float32).astype(jnp.bfloat16)
    act_pred = jnp.einsum("buh,hj->buj", pred_loc, w_pred, preferred_element_type=jnp.float32).astype(jnp.bfloat16)
    hidden = jnp.tanh(act_enc.astype(jnp.float32)[:, :, None, :] + act_pred.astype(jnp.float32)[:, None, :, :]).astype(jnp.bfloat16)
    logits = jnp.einsum("btuj,jv->btuv", hidden, w_out, preferred_element_type=jnp.float32)
    log_norm = jax.nn.logsumexp(logits, axis=-1)
    w_label = jnp.take(w_out, lab_ids, axis=1)
    label_logit = jnp.einsum("btuj,jbu->btu", hidden, w_label, preferred_element_type=jnp.float32)
    return hidden, logits, log_norm, logits[..., 0] - log_norm, label_logit - log_norm


def alpha_rows(row_in, blank, lab_cum):
    def frame_step(carry, frame_in):
        blank_t, cum_t = frame_in
        alpha_t = cum_t + lax.cumlogsumexp(carry - cum_t, axis=1)
        return alpha_t + blank_t, alpha_t

    row_out, alpha = lax.scan(frame_step, row_in, (jnp.swapaxes(blank, 0, 1), jnp.swapaxes(lab_cum, 0, 1)))
    return row_out, jnp.swapaxes(alpha, 0, 1)


def beta_rows(row_in, blank, lab_cum, frame_ok, upos_ok, end_row):
    def frame_step(carry, frame_in):
        blank_t, cum_t, valid_t = frame_in
        terms = jnp.where(upos_ok, carry + blank_t + cum_t, NEG_FILL)
        beta_t = jnp.where(upos_ok, lax.cumlogsumexp(terms, axis=1, reverse=True) - cum_t, NEG_FILL)
        beta_t = jnp.where(valid_t[:, None], beta_t, end_row)
        return beta_t, beta_t

    row_out, beta = lax.scan(frame_step, row_in, (jnp.swapaxes(blank, 0, 1), jnp.swapaxes(lab_cum, 0, 1), frame_ok.T), reverse=True)
    return row_out, jnp.swapaxes(beta, 0, 1)


def occupancies(alpha, beta, beta_tail, blank, label_lp, log_prob, frame_ok, label_pos, label_len):
    beta_next = jnp.concatenate([beta[:, 1:], beta_tail[:, None]], axis=1)
    beta_right = jnp.concatenate([beta[:, :, 1:], jnp.full(beta.shape[:2] + (1,), NEG_FILL, jnp.float32)], axis=2)
    shift = log_prob[:, None, None]
    cell_ok = frame_ok[:, :, None] & (label_pos[None, None, :] <= label_len[:, None, None])
    label_ok = cell_ok & (label_pos[None, None, :] < label_len[:, None, None])
    occ_blank = jnp.where(cell_ok, jnp.exp(alpha + blank + beta_next - shift), 0.0)
    occ_label = jnp.where(label_ok, jnp.exp(alpha + label_lp + beta_right - shift), 0.0)
    return occ_blank, occ_label


def joint_backward(enc_loc, hidden, logits, log_norm, lab_ids, occ_blank, occ_label, w_enc, w_out):
    vocab = jnp.arange(w_out.shape[1])
    softmax_p = jnp.exp(logits - log_norm[..., None])
    grad_logits = (softmax_p * (occ_blank + occ_label)[..., None] - jnp.where(vocab == 0, occ_blank[..., None], 0.0) - jnp.where(vocab == lab_ids[:, None, :, None], occ_label[..., None], 0.0)).astype(jnp.bfloat16)
    grad_hidden = jnp.einsum("btuv,jv->btuj", grad_logits, w_out, preferred_element_type=jnp.float32)
    grad_w_out = jnp.einsum("btuj,btuv->jv", hidden, grad_logits, preferred_element_type=jnp.float32)
    grad_pre = grad_hidden * (1.0 - jnp.square(hidden.astype(jnp.float32)))
    grad_act_enc = jnp.sum(grad_pre, axis=2).astype(jnp.bfloat16)
    grad_enc = jnp.einsum("btj,hj->bth", grad_act_enc, w_enc, preferred_element_type=jnp.float32).astype(jnp.bfloat16)
    grad_w_enc = jnp.einsum("bth,btj->hj", enc_loc, grad_act_enc, preferred_element_type=jnp.float32)
    return grad_enc, grad_w_enc, grad_w_out, jnp.sum(grad_pre, axis=1)


def solution(mesh):
    n_seq = mesh.shape["seq"]
    to_right = [(src, src + 1) for src in range(n_seq - 1)]
    to_left = [(src + 1, src) for src in range(n_seq - 1)]
    utt_rows = P(("part", "data"))
    utt_mats = P(("part", "data"), None)
    utt_cube = P(("part", "data"), None, None)
    enc_spec = P(("part", "data"), "seq", None)
    weight_in = P(None, None)
    weight_out = P("part", None)

    def body(enc_loc, pred_loc, w_enc, w_pred, w_out, labels, frame_len, label_len):
        n_utt, t_loc, _ = enc_loc.shape
        n_upos = pred_loc.shape[1]
        seq_pos = lax.axis_index("seq")
        lab_ids = jnp.concatenate([labels, jnp.zeros((n_utt, 1), jnp.int32)], axis=1)
        hidden, logits, log_norm, blank, label_lp = joint_forward(enc_loc, pred_loc, w_enc, w_pred, w_out, lab_ids)
        lab_cum = jnp.concatenate([jnp.zeros((n_utt, t_loc, 1), jnp.float32), jnp.cumsum(label_lp[:, :, :-1], axis=2)], axis=2)
        label_pos = jnp.arange(n_upos)
        frame_pos = seq_pos * t_loc + jnp.arange(t_loc)
        frame_ok = frame_pos[None, :] < frame_len[:, None]
        upos_ok = label_pos[None, :] <= label_len[:, None]
        start_row = jnp.broadcast_to(jnp.where(label_pos == 0, 0.0, NEG_FILL), (n_utt, n_upos)).astype(jnp.float32)
        end_row = jnp.where(label_pos[None, :] == label_len[:, None], 0.0, NEG_FILL).astype(jnp.float32)

        def alpha_hop(hop_idx, row_in):
            row_out, _ = alpha_rows(row_in, blank, lab_cum)
            received = lax.ppermute(row_out, "seq", to_right)
            return jnp.where(seq_pos == 0, start_row, received)

        alpha_in = lax.fori_loop(0, n_seq - 1, alpha_hop, start_row)
        _, alpha = alpha_rows(alpha_in, blank, lab_cum)
        last_cell = (frame_pos[None, :, None] == frame_len[:, None, None] - 1) & (label_pos[None, None, :] == label_len[:, None, None])
        log_prob = lax.psum(jnp.sum(jnp.where(last_cell, alpha + blank, 0.0), axis=(1, 2)), "seq")

        def beta_hop(hop_idx, row_in):
            row_out, _ = beta_rows(row_in, blank, lab_cum, frame_ok, upos_ok, end_row)
            received = lax.ppermute(row_out, "seq", to_left)
            return jnp.where(seq_pos == n_seq - 1, end_row, received)

        beta_in = lax.fori_loop(0, n_seq - 1, beta_hop, end_row)
        _, beta = beta_rows(beta_in, blank, lab_cum, frame_ok, upos_ok, end_row)
        occ_blank, occ_label = occupancies(alpha, beta, beta_in, blank, label_lp, log_prob, frame_ok, label_pos, label_len)
        grad_enc, grad_w_enc, grad_w_out, act_pred_part = joint_backward(enc_loc, hidden, logits, log_norm, lab_ids, occ_blank, occ_label, w_enc, w_out)
        act_pred_grad = lax.psum(act_pred_part, "seq").astype(jnp.bfloat16)
        grad_pred = jnp.einsum("buj,hj->buh", act_pred_grad, w_pred, preferred_element_type=jnp.float32)
        grad_w_pred = jnp.einsum("buh,buj->hj", pred_loc, act_pred_grad, preferred_element_type=jnp.float32)
        grad_w_enc = lax.psum(grad_w_enc, ("data", "seq"))
        grad_w_out = lax.psum(grad_w_out, ("data", "seq"))
        grad_w_pred = lax.psum(grad_w_pred, "data")
        return -log_prob, grad_enc, grad_pred, grad_w_enc, grad_w_pred, grad_w_out

    return jax.shard_map(body, mesh=mesh, in_specs=(enc_spec, utt_cube, weight_in, weight_in, weight_in, utt_mats, utt_rows, utt_rows), out_specs=(utt_rows, enc_spec, utt_cube, weight_out, weight_out, weight_out), check_vma=False)
```

profile of v0, /device:TPU:97, one launch (start us, length us, event | category | flops | bytes accessed | tf_op | source)
XLA Modules:
  0.0 635.6 jit_solution(12633757343824387502)
XLA Ops:
  10.2 8.0 %copy.44 = bf16[640,4096]{0,1:T(8,128)(2,1)} copy(bf16[640,4096]{1,0:T(8,128)(2,1)} %param.24) | data formatting | bytes 10485760 | tf_op args[4]
  18.2 1.6 fusion.35
  19.8 1.8 fusion.33
  22.7 4.1 tanh_convert_fusion
  26.8 32.5 %fusion.54 = (f32[16,8,32]{2,1,0:T(8,128)S(1)}, f32[16,8,32,4096]{3,2,1,0:T(8,128)}) fusion(bf16[640,4096]{1,0:T(8,128)(2,1)S(1)} %bitcast.200, f32[16,32,640]{2,1,0:T(8,128)} %copy-done.1, f32[16,8,640]{2,1,0:T(8,128)S(1)} %fusion.35), kind=kOutput, calls=%fused_computation.110 | convolution fusion | flops 21496852480 | bytes 74006528 | tf_op jit(solution)/shard_map/btuj,jv->btuv/dot_general | solution.py:13
  59.4 5.3 gather_fusion
  64.9 6.0 fusion.27
  71.0 21.1 %exponential_reduce_fusion = f32[16,8,32]{2,1,0:T(8,128)S(1)} fusion(f32[16,8,32,4096]{3,2,1,0:T(8,128)} %get-tuple-element.907, f32[16,8,32]{2,1,0:T(8,128)S(1)} %is-finite_select_fusion), kind=kLoop, calls=%fused_computation.42 | loop fusion | flops 33550336 | bytes 67141632 | tf_op jit(solution)/shard_map/reduce_sum | solution.py:14
  92.2 3.0 reduce_window_sum.11
  95.2 2.2 slice_reduce_fusion
  97.7 128.4 %while.108 = (s32[]{:T(128)}, f32[16,32]{1,0:T(8,128)S(1)}, pred[]{:T(512)}, f32[16,8,32]{2,0,1:T(8,128)S(1)}, f32[16,8,32]{2,0,1:T(8,128)S(1)}, /*index=5*/s32[...) while((s32[]{:T(128)}, f32[16,32]{1,0:T(8,128)S(1)}, ...), condition=%wide.region_17.18_spmd.clone.clone, body=%wide.region_13.17_spmd.clone.clone.sunk | while | flops 133253 | bytes 37199 | solution.py:106
  98.1 12.9 %while.111 = (s32[]{:T(128)}, f32[16,32]{1,0:T(8,128)S(1)}, pred[8,16]{1,0:T(8,128)(4,1)S(1)}, f32[8,16,32]{2,1,0:T(8,128)S(1)}, f32[8,16,32]{2,1,0:T(8,128)S(1)...) while((s32[]{:T(128)}, f32[16,32]{1,0:T(8,128)S(1)}, ...), condition=%wide.region_16.16_spmd, body=%wide.region_14.15_spmd.sunk | while | flops 130051 | bytes 21681 | solution.py:38
  111.0 4.0 collective-permute-start
  115.0 2.0 collective-permute-done
  117.2 12.9 %while.111 = (s32[]{:T(128)}, f32[16,32]{1,0:T(8,128)S(1)}, pred[8,16]{1,0:T(8,128)(4,1)S(1)}, f32[8,16,32]{2,1,0:T(8,128)S(1)}, f32[8,16,32]{2,1,0:T(8,128)S(1)...) while((s32[]{:T(128)}, f32[16,32]{1,0:T(8,128)S(1)}, ...), condition=%wide.region_16.16_spmd, body=%wide.region_14.15_spmd.sunk | while | flops 130051 | bytes 21681 | solution.py:38
  130.1 1.9 collective-permute-start
  132.1 3.0 collective-permute-done
  135.4 12.9 %while.111 = (s32[]{:T(128)}, f32[16,32]{1,0:T(8,128)S(1)}, pred[8,16]{1,0:T(8,128)(4,1)S(1)}, f32[8,16,32]{2,1,0:T(8,128)S(1)}, f32[8,16,32]{2,1,0:T(8,128)S(1)...) while((s32[]{:T(128)}, f32[16,32]{1,0:T(8,128)S(1)}, ...), condition=%wide.region_16.16_spmd, body=%wide.region_14.15_spmd.sunk | while | flops 130051 | bytes 21681 | solution.py:38
  148.3 1.9 collective-permute-start
  150.3 3.0 collective-permute-done
  153.6 12.9 %while.111 = (s32[]{:T(128)}, f32[16,32]{1,0:T(8,128)S(1)}, pred[8,16]{1,0:T(8,128)(4,1)S(1)}, f32[8,16,32]{2,1,0:T(8,128)S(1)}, f32[8,16,32]{2,1,0:T(8,128)S(1)...) while((s32[]{:T(128)}, f32[16,32]{1,0:T(8,128)S(1)}, ...), condition=%wide.region_16.16_spmd, body=%wide.region_14.15_spmd.sunk | while | flops 130051 | bytes 21681 | solution.py:38
  166.5 1.9 collective-permute-start
  168.4 3.0 collective-permute-done
  171.8 12.9 %while.111 = (s32[]{:T(128)}, f32[16,32]{1,0:T(8,128)S(1)}, pred[8,16]{1,0:T(8,128)(4,1)S(1)}, f32[8,16,32]{2,1,0:T(8,128)S(1)}, f32[8,16,32]{2,1,0:T(8,128)S(1)...) while((s32[]{:T(128)}, f32[16,32]{1,0:T(8,128)S(1)}, ...), condition=%wide.region_16.16_spmd, body=%wide.region_14.15_spmd.sunk | while | flops 130051 | bytes 21681 | solution.py:38
  184.7 1.9 collective-permute-start
  186.6 3.0 collective-permute-done
  190.0 12.9 %while.111 = (s32[]{:T(128)}, f32[16,32]{1,0:T(8,128)S(1)}, pred[8,16]{1,0:T(8,128)(4,1)S(1)}, f32[8,16,32]{2,1,0:T(8,128)S(1)}, f32[8,16,32]{2,1,0:T(8,128)S(1)...) while((s32[]{:T(128)}, f32[16,32]{1,0:T(8,128)S(1)}, ...), condition=%wide.region_16.16_spmd, body=%wide.region_14.15_spmd.sunk | while | flops 130051 | bytes 21681 | solution.py:38
  202.8 1.9 collective-permute-start
  204.8 3.0 collective-permute-done
  208.1 12.9 %while.111 = (s32[]{:T(128)}, f32[16,32]{1,0:T(8,128)S(1)}, pred[8,16]{1,0:T(8,128)(4,1)S(1)}, f32[8,16,32]{2,1,0:T(8,128)S(1)}, f32[8,16,32]{2,1,0:T(8,128)S(1)...) while((s32[]{:T(128)}, f32[16,32]{1,0:T(8,128)S(1)}, ...), condition=%wide.region_16.16_spmd, body=%wide.region_14.15_spmd.sunk | while | flops 130051 | bytes 21681 | solution.py:38
  221.0 1.9 collective-permute-start
  223.0 3.0 collective-permute-done
  226.1 14.5 %while.109 = (s32[]{:T(128)}, f32[16,32]{1,0:T(8,128)S(1)}, f32[8,16,32]{2,0,1:T(8,128)S(1)}, pred[8,16]{1,0:T(8,128)(4,1)S(1)}, f32[8,16,32]{2,1,0:T(8,128)S(1)...) while((s32[]{:T(128)}, f32[16,32]{1,0:T(8,128)S(1)}, ...), condition=%wide.region_20.21_spmd.clone.clone, body=%wide.region_18.20_spmd.clone.clone.sunk | while | flops 135171 | bytes 29073 | solution.py:38
  226.2 1.5 reduce_window.50
  228.0 1.5 reduce_window.50
  229.8 1.5 reduce_window.50
  240.8 3.0 iota_compare_fusion.4
  243.8 76.9 %while.106 = (s32[]{:T(128)}, f32[16,32]{1,0:T(8,128)S(1)}, pred[]{:T(512)}, f32[16,8,32]{2,0,1:T(8,128)S(1)}, f32[16,8,32]{2,0,1:T(8,128)S(1)}, /*index=5*/f32[...) while((s32[]{:T(128)}, f32[16,32]{1,0:T(8,128)S(1)}, pred[]{:T(512)}, ...), condition=%wide.region_7.8_spmd.clone, body=%wide.region_3.7_spmd.clone.sunk | while | flops 129028 | bytes 31135 | solution.py:96
  243.8 6.3 while.110
  250.1 2.0 collective-permute-start.1
  253.2 6.3 while.110
  259.5 3.9 collective-permute-start.1
  264.1 6.3 while.110
  270.4 4.2 collective-permute-start.1
  275.5 6.3 while.110
  281.7 4.2 collective-permute-start.1
  286.8 6.3 while.110
  293.1 4.2 collective-permute-start.1
  298.1 6.3 while.110
  304.4 4.2 collective-permute-start.1
  309.4 6.3 while.110
  315.7 4.2 collective-permute-start.1
  320.7 6.9 %while.104 = (s32[]{:T(128)}, f32[16,32]{1,0:T(8,128)S(1)}, f32[8,16,32]{2,0,1:T(8,128)S(1)}, f32[8,16,32]{2,1,0:T(8,128)S(1)}, f32[8,16,32]{2,1,0:T(8,128)S(1)}, /*index=5*/s32[]{:T(128)}, f32[]{:T(128)}, s32[]{:T(128)}) while((s32[]{:T(128)}, f32[16,32]{1,0:T(8,128)S(1)}, f32[8,16,32]{2,0,1:T(8,128)S(1)}, f32[8,16,32]{2,1,0:T(8,128)S(1)}, ...), condition=%wide.region_10.11_spmd, body=%wide.region_8.10_spmd.sunk | while | flops 129026 | bytes 28785 | solution.py:26
  327.9 13.4 %psum.35 = f32[16]{0:T(128)S(1)} all-reduce(f32[16]{0:T(128)S(1)} %select_reduce_fusion), channel_id=1, replica_groups=mesh['part'=1,'data'=4,'seq'=8] {'seq'}, use_global_device_ids=true, to_apply=%region_12.13 | all-reduce | flops 16 | bytes 128 | tf_op jit(solution)/shard_map/psum | solution.py:99
  341.4 46.8 %fusion.21 = (f32[16,32,640]{2,1,0:T(8,128)}, bf16[16,8,640]{2,1,0:T(8,128)(2,1)}) fusion(f32[16,32,640]{2,1,0:T(8,128)S(1)} %copy-done.2, f32[16,8,640]{2,1,0:T(8,128)S(1)} %fusion.35, bf16[640,4096]{1,0:T(8,128)(2,1)} %param.24, f32[16,8,32,4096]{3,2,1,0:T(8,128)} %get-tuple-element.907, f32[16,8,32]{2,1,0:T(8,128)S(1)} %get-tuple-element.896, ...), kind=kOutput, calls=%fused_computation.47 | convolution fusion | flops 21612838912 | bytes 77631488 | tf_op jit(solution)/shard_map/btuv,jv->btuj/dot_general | solution.py:57
  388.2 51.4 %all-reduce.11 = bf16[16,32,640]{2,1,0:T(8,128)(2,1)S(1)} all-reduce(f32[16,32,640]{2,1,0:T(8,128)} %get-tuple-element.816), channel_id=1, replica_groups=mesh['part'=1,'data'=4,'seq'=8] {'seq'}, use_global_device_ids=true, to_apply=%region_23.24 | all-reduce | flops 327680 | bytes 1966080 | tf_op jit(solution)/shard_map/psum | solution.py:110
  439.6 3.0 convolution_bitcast_fusion.1
  442.8 43.8 %convolution_bitcast_fusion = f32[640,4096]{1,0:T(8,128)} fusion(f32[16,32,640]{2,1,0:T(8,128)S(1)} %copy-done.2, f32[16,8,640]{2,1,0:T(8,128)S(1)} %fusion.35, f32[16,8,32,4096]{3,2,1,0:T(8,128)} %get-tuple-element.907, f32[16,8,32]{2,1,0:T(8,128)} %copy-done.9, f32[16,8,32]{2,1,0:T(8,128)S(1)} %get-tuple-element.895, ...), kind=kOutput, calls=%fused_computation.46 | convolution fusion | flops 21597519872 | bytes 81399808 | tf_op jit(solution)/shard_map/btuj,btuv->jv/dot_general | solution.py:58
  486.6 1.6 convolution_bitcast_fusion.2
  489.8 1.8 fusion.36
  492.6 2.7 copy.58
  495.3 121.4 %all-reduce.10.cloned.1.call-done = (f32[640,640]{0,1:T(8,128)}, f32[640,4096]{1,0:T(8,128)}) async-done(((f32[640,640]{0,1:T(8,128)}, f32[640,4096]{1,0:T(8,128)}), (f32[640,640]{0,1:T(8,128)}, f32[640,4096]{1,0:T(8,128)})) %all-reduce.10.cloned.1.call-update) | async-done | bytes 12124176 | tf_op jit(solution)/shard_map/psum | solution.py:113
  616.7 2.7 copy.57
  619.4 9.3 %copy.136 = f32[640,4096]{1,0:T(8,128)} copy(f32[640,4096]{1,0:T(8,128)} %get-tuple-element.1343) | data formatting | bytes 20971520
  (584 shorter events, 165.6 us)
Async XLA Ops:
  7.2 12.6 %copy-start = (bf16[640,640]{1,0:T(8,128)(2,1)S(1)}, bf16[640,640]{1,0:T(8,128)(2,1)}, u32[]{:S(2)}) copy-start(bf16[640,640]{1,0:T(8,128)(2,1)} %param.23) | copy-start | bytes 2457604
  7.2 11.0 %copy-start.5 = (bf16[16,8,640]{2,1,0:T(8,128)(2,1)S(1)}, bf16[16,8,640]{2,1,0:T(8,128)(2,1)}, u32[]{:S(2)}) copy-start(bf16[16,8,640]{2,1,0:T(8,128)(2,1)} %param.20) | copy-start | bytes 491524
  7.2 485.4 %all-reduce.8.cloned.1.call-start = ((), (), s32[]{:S(2)}) async-start(), calls=%async_computation | async-start | bytes 3276800 | tf_op jit(solution)/shard_map/psum | solution.py:115
  10.2 16.6 %slice-start = ((s8[5242880]{0:T(1024)(128)(4,1)}), s8[1048576]{0:T(1024)(128)(4,1)S(1)}, s32[]{:S(2)}) async-start(s8[5242880]{0:T(1024)(128)(4,1)} %bitcast.199), calls=%async_computation.2 | async-start | bytes 2097152
  18.2 8.6 %slice-start.1 = ((s8[5242880]{0:T(1024)(128)(4,1)}), s8[4194304]{0:T(1024)(128)(4,1)S(1)}, s32[]{:S(2)}) async-start(s8[5242880]{0:T(1024)(128)(4,1)} %bitcast.199), calls=%async_computation.3 | async-start | bytes 8388608
  21.7 1.1 copy-start.1
  71.0 26.5 %copy-start.10 = (s32[16]{0:T(128)S(1)}, s32[16]{0:T(128)}, u32[]{:S(2)}) copy-start(s32[16]{0:T(128)} %param.26) | copy-start | bytes 196
  71.0 26.7 %copy-start.4 = (s32[16]{0:T(128)S(1)}, s32[16]{0:T(128)}, u32[]{:S(2)}) copy-start(s32[16]{0:T(128)} %param.27) | copy-start | bytes 196
  92.1 249.2 %copy-start.2 = (f32[16,32,640]{2,1,0:T(8,128)S(1)}, f32[16,32,640]{2,1,0:T(8,128)}, u32[]{:S(2)}) copy-start(f32[16,32,640]{2,1,0:T(8,128)} %copy-done.1) | copy-start | bytes 3932164
  111.0 5.9 collective-permute-start
  130.1 5.0 collective-permute-start
  148.3 5.0 collective-permute-start
  166.5 5.0 collective-permute-start
  184.7 5.0 collective-permute-start
  202.8 5.0 collective-permute-start
  221.0 5.0 collective-permute-start
  250.1 3.1 collective-permute-start.1
  259.5 4.7 collective-permute-start.1
  270.4 5.0 collective-permute-start.1
  281.7 5.0 collective-permute-start.1
  293.1 5.0 collective-permute-start.1
  304.4 5.0 collective-permute-start.1
  315.7 5.0 collective-permute-start.1
  341.4 46.8 %copy-start.9 = (f32[16,8,32]{2,1,0:T(8,128)}, f32[16,8,32]{2,1,0:T(8,128)S(1)}, u32[]{:S(2)}) copy-start(f32[16,8,32]{2,1,0:T(8,128)S(1)} %get-tuple-element.896) | copy-start | bytes 49156
  442.7 43.9 %copy-start.6 = (bf16[16,8,640]{2,1,0:T(8,128)(2,1)S(1)}, bf16[16,8,640]{2,1,0:T(8,128)(2,1)}, u32[]{:S(2)}) copy-start(bf16[16,8,640]{2,1,0:T(8,128)(2,1)} %param.20) | copy-start | bytes 491524
  442.7 174.0 %all-reduce.10.cloned.1.call-start = ((), (), s32[]{:S(2)}) async-start(), calls=%async_computation.1 | async-start | bytes 24248320 | tf_op jit(solution)/shard_map/psum | solution.py:113
  442.7 43.8 %copy-start.7 = (bf16[16,8,640]{2,1,0:T(8,128)(2,1)S(1)}, bf16[16,8,640]{2,1,0:T(8,128)(2,1)}, u32[]{:S(2)}) copy-start(bf16[16,8,640]{2,1,0:T(8,128)(2,1)} %get-tuple-element.817) | copy-start | bytes 491524
  486.6 2.2 copy-start.3
  486.6 2.2 copy-start.8
Sparse Core Ops, SparseCore 0:
  442.8 49.7 all-reduce.7
  496.8 119.7 all-reduce.9
where the time goes:
time: 637 us; the launch traced here: 636 us
  other arithmetic  190 us (30%)
  waiting for transfers between devices  148 us (23%)
  matrix products  140 us (22%)
  blocking collectives  64.8 us (10%)
  starting transfers between devices  42.8 us (7%)
  local copies, waits for them, and re-layouts  33.2 us (5%)
  between operations  14.4 us (2%)
    psum x1, waiting for transfers between devices, body(): grad_w_enc = lax.psum(grad_w_enc, ('data', 'seq'))  121 us
    another operation x64, other arithmetic, frame_step(): lax.cumlogsumexp(terms, axis=1, reverse=True) - cum_t  96 us
    psum x1, blocking collectives, body(): act_pred_grad = lax.psum(act_pred_part, 'seq').astype(jnp.bfloat16)  51.4 us
    another operation x64, other arithmetic, frame_step(): alpha_t = cum_t + lax.cumlogsumexp(carry - cum_t, axis=1)  49.1 us
    dot_general x1, matrix products, joint_backward(): jnp.einsum('btuv,jv->btuj', grad_logits, w_out, preferred_element_type=jn...  46.8 us
    dot_general x1, matrix products, joint_backward(): jnp.einsum('btuj,btuv->jv', hidden, grad_logits, preferred_element_type=j...  43.8 us
    dot_general x1, matrix products, joint_forward(): jnp.einsum('btuj,jv->btuv', hidden, w_out, preferred_element_type=jnp.flo...  32.5 us
    ppermute x7, starting transfers between devices, alpha_hop(): received = lax.ppermute(row_out, 'seq', to_right)  27 us
  transfers between devices with their start and end apart: 16, of which 16 were waited for; matrix products, arithmetic and copies ran while one was open for 8% of the time, Pallas kernels for 0%

commit v1 on v0

v1 whole, which is shorter than its diff:
```python
import functools

import jax
import jax.numpy as jnp
from jax import lax
from jax.experimental import pallas as pl
from jax.experimental.pallas import tpu as pltpu
from jax.sharding import PartitionSpec as P

NEG_FILL = -1e30
LANES = 128
SUB = 8
TILE_F = 256
TILE_B = 512
CHUNK = 512
F32 = jnp.float32
BF16 = jnp.bfloat16


def frame_of(dev, idx, n_seq, t_loc):
    return dev * t_loc + idx


def fwd_kernel(n_utt, t_loc, n_upos, nt_ref, nk_ref, enc_ref, pred_ref, wenc_ref, wpred_ref, w_ref, lab_ref,
               z_hbm, h_hbm, stat_ref, act_e, act_p, hf, labr, rstat, zbuf, hbuf, m_s, s_s, l_s, zsem, hsem):
    vocab = w_ref.shape[1]
    act_e[...] = jnp.dot(enc_ref[...], wenc_ref[...], preferred_element_type=F32).astype(BF16).astype(F32)
    act_p[...] = jnp.dot(pred_ref[...], wpred_ref[...], preferred_element_type=F32).astype(BF16).astype(F32)

    def per_utt(b, base):
        n_t = nt_ref[b]
        a_utt = act_e[pl.ds(pl.multiple_of(b * t_loc, SUB), t_loc), :]

        def per_k(k, base):
            row = pl.multiple_of(b * n_upos + k * SUB, SUB)
            c_k = act_p[pl.ds(row, SUB), :]
            lab_k = lab_ref[pl.ds(row, SUB), :]
            for i in range(t_loc):
                dst = pl.ds(pl.multiple_of((base + i) * SUB, SUB), SUB)
                hf[dst, :] = jnp.tanh(a_utt[i:i + 1, :] + c_k)
                labr[dst, :] = lab_k
            return base + n_t

        return lax.fori_loop(0, jnp.where(n_t > 0, nk_ref[b], 0), per_k, base)

    total = lax.fori_loop(0, n_utt, per_utt, 0)
    n_tiles = pl.cdiv(total * SUB, TILE_B) * (TILE_B // TILE_F)

    def clear(r, _):
        dst = pl.ds(pl.multiple_of((total + r) * SUB, SUB), SUB)
        hf[dst, :] = jnp.zeros((SUB, hf.shape[1]), F32)
        labr[dst, :] = jnp.full((SUB, LANES), -1, jnp.int32)
        return 0

    lax.fori_loop(0, n_tiles * (TILE_F // SUB) - total, clear, 0)

    def out_copies(n, slot):
        rows = pl.ds(pl.multiple_of(n * TILE_F, TILE_F), TILE_F)
        return (pltpu.make_async_copy(zbuf.at[slot], z_hbm.at[rows, :], zsem.at[slot]),
                pltpu.make_async_copy(hbuf.at[slot], h_hbm.at[rows, :], hsem.at[slot]))

    def tile(n, _):
        slot = lax.rem(n, 2)

        @pl.when(n >= 2)
        def _():
            for cp in out_copies(n - 2, slot):
                cp.wait()

        row0 = pl.multiple_of(n * TILE_F, TILE_F)
        hb = hf[pl.ds(row0, TILE_F), :].astype(BF16)
        hbuf[slot] = hb
        lane = lax.broadcasted_iota(jnp.int32, (1, LANES), 1)
        grp = 32
        for c in range(vocab // CHUNK):
            zbuf[slot, :, c * CHUNK:(c + 1) * CHUNK] = jnp.dot(hb, w_ref[:, c * CHUNK:(c + 1) * CHUNK], preferred_element_type=F32)
            for r in range(0, TILE_F, grp):
                rs = slice(r, r + grp)
                zk = [zbuf[slot, rs, c * CHUNK + q * LANES:c * CHUNK + (q + 1) * LANES] for q in range(CHUNK // LANES)]
                lab = labr[pl.ds(row0 + r, grp), :]
                mx = functools.reduce(jnp.maximum, zk)
                if c > 0:
                    m_old = m_s[rs, :]
                    mx = jnp.maximum(mx, m_old)
                sm = functools.reduce(jnp.add, [jnp.exp(z - mx) for z in zk])
                lz = functools.reduce(jnp.add, [jnp.where(lab == lane + (c * CHUNK + q * LANES), z, 0.0) for q, z in enumerate(zk)])
                if c > 0:
                    sm = sm + s_s[rs, :] * jnp.exp(m_old - mx)
                    lz = lz + l_s[rs, :]
                m_s[rs, :] = mx
                s_s[rs, :] = sm
                l_s[rs, :] = lz
        for cp in out_copies(n, slot):
            cp.start()
        for r in range(0, TILE_F, grp):
            rs = slice(r, r + grp)
            dst = pl.ds(row0 + r, grp)
            m_l = m_s[rs, :]
            m_r = jnp.max(m_l, axis=1, keepdims=True)
            s_r = jnp.sum(s_s[rs, :] * jnp.exp(m_l - m_r), axis=1, keepdims=True)
            lse = m_r + jnp.log(s_r)
            rstat[0, dst, :] = jnp.broadcast_to(lse, (grp, LANES))
            rstat[1, dst, :] = jnp.broadcast_to(zbuf[slot, rs, 0:1] - lse, (grp, LANES))
            rstat[2, dst, :] = jnp.broadcast_to(jnp.sum(l_s[rs, :], axis=1, keepdims=True) - lse, (grp, LANES))
        return 0

    lax.fori_loop(0, n_tiles, tile, 0)

    stat_ref[...] = jnp.zeros_like(stat_ref)
    lane8 = lax.broadcasted_iota(jnp.int32, (SUB, LANES), 1)

    def utt_out(b, base):
        n_t = nt_ref[b]

        def k_out(k, base):
            us = pl.ds(pl.multiple_of(k * SUB, SUB), SUB)
            acc = [stat_ref[s, us, :] for s in range(3)]
            for i in range(t_loc):
                src = pl.ds(pl.multiple_of((base + i) * SUB, SUB), SUB)
                hit = lane8 == jnp.where(i < n_t, i * n_utt + b, -1)
                acc = [jnp.where(hit, rstat[s, src, :], acc[s]) for s in range(3)]
            for s in range(3):
                stat_ref[s, us, :] = acc[s]
            return base + n_t

        return lax.fori_loop(0, jnp.where(n_t > 0, nk_ref[b], 0), k_out, base)

    lax.fori_loop(0, n_utt, utt_out, 0)

    @pl.when(n_tiles > 0)
    def _():
        for back in (2, 1):
            for cp in out_copies(n_tiles - back, lax.rem(n_tiles - back, 2)):
                cp.wait()


def log_add(x, y):
    return jnp.maximum(x, y) + jnp.log(1.0 + jnp.exp(-jnp.abs(x - y)))


def lattice_kernel(n_seq, t_loc, n_utt, stat_ref, len_ref, q_ref, logp_ref, gath, bsk, lsk, asv, xsv, ysv, send_sem, recv_sem):
    me = lax.axis_index("seq")
    n_upos = stat_ref.shape[1]
    n_diag = bsk.shape[0] // n_upos
    skew = n_upos + 1
    barrier = pltpu.get_barrier_semaphore()
    for p in range(1, n_seq):
        pl.semaphore_signal(barrier, inc=1, device_id={"seq": lax.rem(me + p, n_seq)}, device_id_type=pl.DeviceIdType.MESH)
    pl.semaphore_wait(barrier, n_seq - 1)
    copies = []
    for p in range(1, n_seq):
        cp = pltpu.make_async_remote_copy(
            src_ref=stat_ref.at[pl.ds(1, 2)], dst_ref=gath.at[me], send_sem=send_sem.at[p], recv_sem=recv_sem.at[p],
            device_id={"seq": lax.rem(me + p, n_seq)}, device_id_type=pl.DeviceIdType.MESH)
        cp.start()
        copies.append(cp)
    gath[me] = stat_ref[1:3]
    fill = jnp.full((n_upos, LANES), NEG_FILL, F32)

    def clear(d, _):
        row = pl.ds(pl.multiple_of(d * n_upos, n_upos), n_upos)
        bsk[row, :] = fill
        lsk[row, :] = fill
        return 0

    lax.fori_loop(0, n_diag, clear, 0)
    for cp in copies:
        cp.wait()

    upos = lax.broadcasted_iota(jnp.int32, (n_upos, LANES), 0)
    lane = lax.broadcasted_iota(jnp.int32, (n_upos, LANES), 1)
    t_len = len_ref[0:1, :]
    u_len = len_ref[1:2, :]

    def place(dev, _):
        t_lane = frame_of(dev, lane // n_utt, n_seq, t_loc)
        live = (t_lane < t_len) & (upos <= u_len)
        blank = jnp.where(live, gath[dev, 0], NEG_FILL)
        label = jnp.where(live & (upos < u_len), gath[dev, 1], NEG_FILL)
        for i in range(t_loc):
            t = frame_of(dev, i, n_seq, t_loc)
            b_i = blank if i == 0 else pltpu.roll(blank, LANES - i * n_utt, 1)
            l_i = label if i == 0 else pltpu.roll(label, LANES - i * n_utt, 1)
            for k in range(n_upos // SUB):
                rows = pl.ds(t * n_upos + k * SUB * skew, SUB, stride=skew)
                bsk[rows, :] = b_i[k * SUB:(k + 1) * SUB]
                lsk[rows, :] = l_i[k * SUB:(k + 1) * SUB]
        return 0

    lax.fori_loop(0, n_seq, place, 0)

    end_diag = jnp.where(upos == u_len, t_len + u_len, -1)
    first = upos == 0
    last = upos == n_upos - 1

    def step(d, carry):
        alpha, beta, logp = carry
        e = n_diag - 1 - d
        rd = pl.ds(pl.multiple_of(d * n_upos, n_upos), n_upos)
        re = pl.ds(pl.multiple_of(e * n_upos, n_upos), n_upos)
        asv[rd, :] = alpha
        logp = jnp.where(end_diag == d, alpha, logp)
        x = alpha + bsk[rd, :]
        y = jnp.where(first, NEG_FILL, pltpu.roll(alpha + lsk[rd, :], 1, 0))
        xb = beta + bsk[re, :]
        yb = jnp.where(last, NEG_FILL, pltpu.roll(beta, n_upos - 1, 0)) + lsk[re, :]
        xsv[re, :] = xb
        ysv[re, :] = yb
        return log_add(x, y), jnp.where(end_diag == e, 0.0, log_add(xb, yb)), logp

    start = jnp.where(first, 0.0, fill)
    _, _, logp = lax.fori_loop(0, n_diag, step, (start, fill, jnp.zeros_like(fill)))
    logp = jnp.sum(logp, axis=0, keepdims=True)
    logp_ref[...] = logp
    for k in range(n_upos // SUB):
        acc0 = jnp.zeros((SUB, LANES), F32)
        acc1 = jnp.zeros((SUB, LANES), F32)
        for i in range(t_loc):
            t = frame_of(me, i, n_seq, t_loc)
            rows = pl.ds(t * n_upos + k * SUB * skew, SUB, stride=skew)
            al = asv[rows, :] - logp
            occ0 = jnp.exp(al + xsv[rows, :])
            occ1 = jnp.exp(al + ysv[rows, :])
            if i:
                occ0 = pltpu.roll(occ0, i * n_utt, 1)
                occ1 = pltpu.roll(occ1, i * n_utt, 1)
            hit = lane[:SUB] // n_utt == i
            acc0 = jnp.where(hit, occ0, acc0)
            acc1 = jnp.where(hit, occ1, acc1)
        q_ref[0, k * SUB:(k + 1) * SUB, :] = acc0
        q_ref[1, k * SUB:(k + 1) * SUB, :] = acc1


def bwd_kernel(n_utt, t_loc, n_upos, nt_ref, nk_ref, w_ref, lab_ref, stat_ref, q_ref, h_hbm, z_hbm,
               dw_ref, da_ref, dc_ref, rlse, rq0, rq1, labr, dsr, zs, dzb, hbuf, ht, dhs, da_acc, zsem, hsem):
    vocab = w_ref.shape[1]
    half = vocab // 2
    lane8 = lax.broadcasted_iota(jnp.int32, (SUB, LANES), 1)

    def per_utt(b, base):
        n_t = nt_ref[b]

        def per_k(k, base):
            us = pl.ds(pl.multiple_of(k * SUB, SUB), SUB)
            lab_k = lab_ref[pl.ds(pl.multiple_of(b * n_upos + k * SUB, SUB), SUB), :]
            lse_k, q0_k, q1_k = stat_ref[0, us, :], q_ref[0, us, :], q_ref[1, us, :]
            for i in range(t_loc):
                dst = pl.ds(pl.multiple_of((base + i) * SUB, SUB), SUB)
                hit = lane8 == i * n_utt + b
                for ref, val in ((rlse, lse_k), (rq0, q0_k), (rq1, q1_k)):
                    ref[dst, :] = jnp.broadcast_to(jnp.sum(jnp.where(hit, val, 0.0), axis=1, keepdims=True), (SUB, LANES))
                labr[dst, :] = lab_k
            return base + n_t

        return lax.fori_loop(0, jnp.where(n_t > 0, nk_ref[b], 0), per_k, base)

    total = lax.fori_loop(0, n_utt, per_utt, 0)
    n_tiles = pl.cdiv(total * SUB, TILE_B)

    def in_copies(n, part):
        rows = pl.ds(pl.multiple_of(n * TILE_B, TILE_B), TILE_B)
        return pltpu.make_async_copy(z_hbm.at[rows, part * half:(part + 1) * half], zs.at[part], zsem.at[part])

    def h_copy(n):
        return pltpu.make_async_copy(h_hbm.at[pl.ds(pl.multiple_of(n * TILE_B, TILE_B), TILE_B), :], hbuf, hsem)

    @pl.when(n_tiles > 0)
    def _():
        h_copy(0).start()
        in_copies(0, 0).start()
        in_copies(0, 1).start()

    def clear(r, _):
        dst = pl.ds(pl.multiple_of((total + r) * SUB, SUB), SUB)
        for ref in (rlse, rq0, rq1):
            ref[dst, :] = jnp.zeros((SUB, LANES), F32)
        labr[dst, :] = jnp.full((SUB, LANES), -1, jnp.int32)
        return 0

    lax.fori_loop(0, n_tiles * (TILE_B // SUB) - total, clear, 0)

    def zero(r, _):
        dw_ref[pl.ds(pl.multiple_of(r * SUB, SUB), SUB), :] = jnp.zeros((SUB, vocab), F32)
        return 0

    lax.fori_loop(0, dw_ref.shape[0] // SUB, zero, 0)
    dc_ref[...] = jnp.zeros_like(dc_ref)

    def tile(n, _):
        row0 = pl.multiple_of(n * TILE_B, TILE_B)
        nxt = jnp.minimum(n + 1, n_tiles - 1)
        lane = lax.broadcasted_iota(jnp.int32, (1, LANES), 1)
        h_copy(n).wait()
        ht[...] = jnp.transpose(hbuf[...])
        grp = 16
        for part in range(2):
            in_copies(n, part).wait()
            for c in range(half // CHUNK):
                for r in range(0, TILE_B, grp):
                    rs = slice(r, r + grp)
                    src = pl.ds(row0 + r, grp)
                    lse, q0, q1, lab = rlse[src, :], rq0[src, :], rq1[src, :], labr[src, :]
                    qs = q0 + q1
                    for q in range(CHUNK // LANES):
                        loc = c * CHUNK + q * LANES
                        col = part * half + loc
                        dz = jnp.exp(zs[part, rs, loc:loc + LANES] - lse) * qs
                        if col == 0:
                            dz = dz - jnp.where(lane == 0, q0, 0.0)
                        dz = dz - jnp.where(lab == lane + col, q1, 0.0)
                        dzb[rs, col:col + LANES] = dz.astype(BF16)
                cs = slice(part * half + c * CHUNK, part * half + (c + 1) * CHUNK)
                dw_ref[:, cs] += jnp.dot(ht[...], dzb[:, cs], preferred_element_type=F32)
            in_copies(nxt, part).start()
            cs = slice(part * half, (part + 1) * half)
            dh = lax.dot_general(dzb[:, cs], w_ref[:, cs], (((1,), (1,)), ((), ())), preferred_element_type=F32)
            if part == 0:
                dhs[...] = dh
            else:
                h32 = hbuf[...].astype(F32)
                dsr[pl.ds(row0, TILE_B), :] = (dhs[...] + dh) * (1.0 - h32 * h32)
        h_copy(nxt).start()
        return 0

    lax.fori_loop(0, n_tiles, tile, 0)

    @pl.when(n_tiles > 0)
    def _():
        h_copy(n_tiles - 1).wait()
        in_copies(n_tiles - 1, 0).wait()
        in_copies(n_tiles - 1, 1).wait()

    def utt_out(b, base):
        n_t = nt_ref[b]
        da_acc[...] = jnp.zeros_like(da_acc)

        def k_out(k, base):
            acc = jnp.zeros((SUB, dsr.shape[1]), F32)
            for i in range(t_loc):
                src = pl.ds(pl.multiple_of((base + i) * SUB, SUB), SUB)
                val = jnp.where(i < n_t, dsr[src, :], 0.0)
                acc = acc + val
                da_acc[i] += val
            dc_ref[pl.ds(pl.multiple_of(b * n_upos + k * SUB, SUB), SUB), :] = acc
            return base + n_t

        base = lax.fori_loop(0, jnp.where(n_t > 0, nk_ref[b], 0), k_out, base)
        for i in range(t_loc):
            da_ref[pl.ds(b * t_loc + i, 1), :] = jnp.sum(da_acc[i], axis=0, keepdims=True)
        return base

    lax.fori_loop(0, n_utt, utt_out, 0)


VMEM = pl.BlockSpec(memory_space=pltpu.VMEM)
SMEM = pl.BlockSpec(memory_space=pltpu.SMEM)
HBM = pl.BlockSpec(memory_space=pl.ANY)
VMEM_LIMIT = 66_000_000


def solution(mesh):
    n_seq = mesh.shape["seq"]
    utt_rows = P(("part", "data"))
    utt_mats = P(("part", "data"), None)
    utt_cube = P(("part", "data"), None, None)
    enc_spec = P(("part", "data"), "seq", None)
    weight_in = P(None, None)
    weight_out = P("part", None)

    def body(enc_loc, pred_loc, w_enc, w_pred, w_out, labels, frame_len, label_len):
        n_utt, t_loc, width = enc_loc.shape
        n_upos = pred_loc.shape[1]
        joint, vocab = w_out.shape
        me = lax.axis_index("seq")
        lab_ids = jnp.concatenate([labels, jnp.zeros((n_utt, 1), jnp.int32)], axis=1)
        lab_b = jnp.broadcast_to(lab_ids.reshape(n_utt * n_upos, 1), (n_utt * n_upos, LANES))
        n_live_t = jnp.sum(frame_of(me, jnp.arange(t_loc), n_seq, t_loc)[None, :] < frame_len[:, None], axis=1, dtype=jnp.int32)
        n_live_k = label_len // SUB + 1
        lens = jnp.stack([jnp.tile(frame_len, LANES // n_utt), jnp.tile(label_len, LANES // n_utt)])
        cells = n_utt * t_loc * n_upos
        rows = cells + t_loc * SUB
        enc2 = enc_loc.reshape(n_utt * t_loc, width)
        pred2 = pred_loc.reshape(n_utt * n_upos, width)

        z, h, stat = pl.pallas_call(
            functools.partial(fwd_kernel, n_utt, t_loc, n_upos),
            out_shape=(jax.ShapeDtypeStruct((cells, vocab), F32), jax.ShapeDtypeStruct((cells, joint), BF16),
                       jax.ShapeDtypeStruct((3, n_upos, LANES), F32)),
            in_specs=[SMEM, SMEM] + [VMEM] * 6,
            out_specs=(HBM, HBM, VMEM),
            scratch_shapes=[
                pltpu.VMEM((n_utt * t_loc, joint), F32), pltpu.VMEM((n_utt * n_upos, joint), F32),
                pltpu.VMEM((rows, joint), F32), pltpu.VMEM((rows, LANES), jnp.int32), pltpu.VMEM((3, rows, LANES), F32),
                pltpu.VMEM((2, TILE_F, vocab), F32), pltpu.VMEM((2, TILE_F, joint), BF16),
                pltpu.VMEM((TILE_F, LANES), F32), pltpu.VMEM((TILE_F, LANES), F32), pltpu.VMEM((TILE_F, LANES), F32),
                pltpu.SemaphoreType.DMA((2,)), pltpu.SemaphoreType.DMA((2,)),
            ],
            compiler_params=pltpu.CompilerParams(vmem_limit_bytes=VMEM_LIMIT),
            name="joint_fwd",
        )(n_live_t, n_live_k, enc2, pred2, w_enc, w_pred, w_out, lab_b)

        n_diag = n_seq * t_loc + n_upos
        sk = pltpu.VMEM((n_diag * n_upos, LANES), F32)
        occ, logp = pl.pallas_call(
            functools.partial(lattice_kernel, n_seq, t_loc, n_utt),
            out_shape=(jax.ShapeDtypeStruct((2, n_upos, LANES), F32), jax.ShapeDtypeStruct((1, LANES), F32)),
            in_specs=[VMEM, VMEM],
            out_specs=(VMEM, VMEM),
            scratch_shapes=[pltpu.VMEM((n_seq, 2, n_upos, LANES), F32), sk, sk, sk, sk, sk,
                            pltpu.SemaphoreType.DMA((n_seq,)), pltpu.SemaphoreType.DMA((n_seq,))],
            compiler_params=pltpu.CompilerParams(collective_id=0, has_side_effects=True, vmem_limit_bytes=VMEM_LIMIT),
            name="lattice",
        )(stat, lens)

        dw_out, da, dc = pl.pallas_call(
            functools.partial(bwd_kernel, n_utt, t_loc, n_upos),
            out_shape=(jax.ShapeDtypeStruct((joint, vocab), F32), jax.ShapeDtypeStruct((n_utt * t_loc, joint), F32),
                       jax.ShapeDtypeStruct((n_utt * n_upos, joint), F32)),
            in_specs=[SMEM, SMEM] + [VMEM] * 4 + [HBM, HBM],
            out_specs=(VMEM, VMEM, VMEM),
            scratch_shapes=[
                pltpu.VMEM((rows, LANES), F32), pltpu.VMEM((rows, LANES), F32), pltpu.VMEM((rows, LANES), F32),
                pltpu.VMEM((rows, LANES), jnp.int32), pltpu.VMEM((rows, joint), F32),
                pltpu.VMEM((2, TILE_B, vocab // 2), F32), pltpu.VMEM((TILE_B, vocab), BF16), pltpu.VMEM((TILE_B, joint), BF16),
                pltpu.VMEM((joint, TILE_B), BF16), pltpu.VMEM((TILE_B, joint), F32), pltpu.VMEM((t_loc, SUB, joint), F32),
                pltpu.SemaphoreType.DMA((2,)), pltpu.SemaphoreType.DMA,
            ],
            compiler_params=pltpu.CompilerParams(vmem_limit_bytes=VMEM_LIMIT),
            name="joint_bwd",
        )(n_live_t, n_live_k, w_out, lab_b, stat, occ, h, z)

        da16 = da.astype(BF16)
        grad_enc = jnp.einsum("rj,hj->rh", da16, w_enc, preferred_element_type=F32).astype(BF16).reshape(enc_loc.shape)
        grad_w_enc = jnp.einsum("rh,rj->hj", enc2, da16, preferred_element_type=F32)
        dc16 = lax.psum(dc, "seq").astype(BF16)
        grad_pred = jnp.einsum("rj,hj->rh", dc16, w_pred, preferred_element_type=F32).reshape(pred_loc.shape)
        grad_w_pred = jnp.einsum("rh,rj->hj", pred2, dc16, preferred_element_type=F32)
        grad_w_enc = lax.psum(grad_w_enc, ("data", "seq"))
        grad_w_out = lax.psum(dw_out, ("data", "seq"))
        grad_w_pred = lax.psum(grad_w_pred, "data")
        return -logp[0, :n_utt], grad_enc, grad_pred, grad_w_enc, grad_w_pred, grad_w_out

    return jax.shard_map(body, mesh=mesh, in_specs=(enc_spec, utt_cube, weight_in, weight_in, weight_in, utt_mats, utt_rows, utt_rows), out_specs=(utt_rows, enc_spec, utt_cube, weight_out, weight_out, weight_out), check_vma=False)
```

time: 637 us -> 397 us (0.62)
  other arithmetic: 190 us -> 3.49 us
  matrix products: 140 us -> 6.31 us
  Pallas kernels: 0 us -> 124 us
  starting transfers between devices: 42.8 us -> 0.13 us
  waiting for transfers between devices: 148 us -> 178 us
  local copies, waits for them, and re-layouts: 33.2 us -> 19 us
  blocking collectives: 64.8 us -> 50.7 us
    another operation x129 -> x1, other arithmetic: 148 us -> 0.57 us  [body(): jnp.stack([jnp.tile(frame_len, LANES // n_utt), jnp.tile(label_len, LANES...]
    dot_general x10 -> x4, matrix products: 140 us -> 6.31 us  [the longest x1 1.87 us: body(): jnp.einsum('rh,rj->hj', pred2, dc16, preferred_element_type=F32)]
    pallas_call x0 -> x3, Pallas kernels: none -> 124 us  [the longest x1 72.4 us: body(): pl.pallas_call(functools.partial(bwd_kernel, n_utt, t_loc, n_upos), out_s...]
    psum x1, waiting for transfers between devices: 0.93 us -> 56.9 us  [body(): grad_w_pred = lax.psum(grad_w_pred, 'data')]
    ppermute x14 -> x0, starting transfers between devices: 42.7 us -> none  [the longest x7 27 us: alpha_hop(): received = lax.ppermute(row_out, 'seq', to_right)]
    ppermute x14 -> x0, waiting for transfers between devices: 26 us -> none  [the longest x7 20.2 us: beta_hop(): received = lax.ppermute(row_out, 'seq', to_left)]
    reduce_sum x2 -> x1, other arithmetic: 21.4 us -> 1.25 us  [body(): jnp.sum(frame_of(me, jnp.arange(t_loc), n_seq, t_loc)[None, :] < frame_le...]
    psum x2 -> x1, blocking collectives: 64.8 us -> 50.7 us  [body(): dc16 = lax.psum(dc, 'seq').astype(BF16)]
  transfers between devices with their start and end apart: 16 -> 2, of which waited for: 16 -> 2; matrix products, arithmetic and copies ran while one was open for 8% -> 2% of each run, Pallas kernels for 0% -> 0%
where the time goes in v1:
time: 397 us; the launch traced here: 396 us
  waiting for transfers between devices  178 us (45%)
  Pallas kernels  124 us (31%)
  blocking collectives  50.7 us (13%)
  local copies, waits for them, and re-layouts  19 us (5%)
  between operations  14.2 us (4%)
  matrix products  6.31 us (2%)
    psum x1, waiting for transfers between devices, body(): grad_w_enc = lax.psum(grad_w_enc, ('data', 'seq'))  121 us
    pallas_call x1, Pallas kernels, body(): pl.pallas_call(functools.partial(bwd_kernel, n_utt, t_loc, n_upos), out_s...  72.4 us
    psum x1, waiting for transfers between devices, body(): grad_w_pred = lax.psum(grad_w_pred, 'data')  56.9 us
    psum x1, blocking collectives, body(): dc16 = lax.psum(dc, 'seq').astype(BF16)  50.7 us
    pallas_call x1, Pallas kernels, body(): pl.pallas_call(functools.partial(fwd_kernel, n_utt, t_loc, n_upos), out_s...  36.7 us
    unnamed x15, local copies, waits for them, and re-layouts  15.9 us
    pallas_call x1, Pallas kernels, body(): pl.pallas_call(functools.partial(lattice_kernel, n_seq, t_loc, n_utt), ou...  15.2 us
  transfers between devices with their start and end apart: 2, of which 2 were waited for; matrix products, arithmetic and copies ran while one was open for 2% of the time, Pallas kernels for 0%

profile of v1, /device:TPU:97, one launch (start us, length us, event | category | flops | bytes accessed | tf_op | source)
XLA Modules:
  0.0 396.4 jit_solution(10619261076918612778)
XLA Ops:
  7.2 0.1 all-reduce.6.cloned.1.call-start
  7.3 1.1 fusion.6.nk_ref
  8.4 0.7 concatenate.3
  9.1 0.1 broadcast_in_dim.4
  9.2 0.7 tile.5
  9.8 0.1 stack_tile.7
  9.9 1.2 convert_reduce_fusion.nt_ref
  11.2 0.7 tile.4
  11.8 0.1 stack_tile.6
  11.9 0.6 pad_add_fusion.len_ref
  12.5 0.8 broadcast_in_dim.10.lab_ref
  13.3 36.7 %joint_fwd.1 = (f32[4096,4096]{1,0:T(8,128)}, bf16[4096,640]{1,0:T(8,128)(2,1)}, f32[3,32,128]{2,1,0:T(8,128)}) custom-call(s32[16]{0:T(128)} %convert_reduce_fusion.nt_ref, s32[16]{0:T(128)} %fusion.6.nk_ref, bf16[128,640]{1,0:T(8,128)(2,1)} %bitcast.21, bf16[512,640]{1,0:T(8,128)(2,1)} %bitcast.18, bf16[640,640]{1,0:T(8,128)(2,1)} %wenc_ref.1, ...), custom_call_target="tpu_custom_call" | custom-call | tf_op jit(solution)/shard_map/joint_fwd/pallas_call | solution.py:385
  50.0 15.2 %lattice.1 = (f32[2,32,128]{2,1,0:T(8,128)}, f32[1,128]{1,0:T(1,128)}) custom-call(f32[3,32,128]{2,1,0:T(8,128)} %get-tuple-element.14.stat_ref, s32[2,128]{1,0:T(2,128)} %pad_add_fusion.len_ref), custom_call_target="tpu_custom_call" | custom-call | tf_op jit(solution)/shard_map/lattice/pallas_call | solution.py:404
  65.2 72.4 %joint_bwd.1 = (f32[640,4096]{1,0:T(8,128)}, f32[128,640]{1,0:T(8,128)}, f32[512,640]{1,0:T(8,128)}) custom-call(s32[16]{0:T(128)} %convert_reduce_fusion.nt_ref, s32[16]{0:T(128)} %fusion.6.nk_ref, bf16[640,4096]{1,0:T(8,128)(2,1)} %w_ref.3, s32[512,128]{1,0:T(8,128)} %broadcast_in_dim.10.lab_ref, f32[3,32,128]{2,1,0:T(8,128)} %get-tuple-element.14.stat_ref, ...), custom_call_target="tpu_custom_call" | custom-call | tf_op jit(solution)/shard_map/joint_bwd/pallas_call | solution.py:415
  137.6 0.0 copy-start.2
  137.6 50.7 %all-reduce.9 = bf16[512,640]{1,0:T(8,128)(2,1)S(1)} all-reduce(f32[512,640]{1,0:T(8,128)} %get-tuple-element.20), channel_id=1, replica_groups=mesh['part'=1,'data'=4,'seq'=8] {'seq'}, use_global_device_ids=true, to_apply=%region_1.2 | all-reduce | flops 327680 | bytes 1966080 | tf_op jit(solution)/shard_map/psum | solution.py:435
  188.3 0.0 copy-done.2
  188.3 0.0 copy-start.3
  188.3 0.0 copy-start.4
  188.3 1.9 convolution_bitcast_fusion
  190.2 0.1 all-reduce.6.cloned.1.call-update
  190.3 0.1 all-reduce.8.cloned.1.call-start
  190.3 0.0 copy-done.3
  190.3 0.0 copy-done.4
  190.4 1.6 convolution_bitcast_fusion.1
  191.9 0.0 copy-start
  191.9 0.0 copy-start.5
  191.9 0.0 copy-start.1
  191.9 0.1 all-reduce.8.cloned.1.call-update
  192.0 1.1 copy-done
  193.1 1.0 fusion
  194.1 0.0 copy-done.5
  194.1 0.5 negate_bitcast_fusion
  194.6 0.0 copy-done.1
  194.6 1.8 fusion.8
  196.5 56.9 %all-reduce.6.cloned.1.call-done = f32[640,640]{0,1:T(8,128)} async-done(((f32[640,640]{0,1:T(8,128)}), f32[640,640]{0,1:T(8,128)}) %all-reduce.6.cloned.1.call-update) | async-done | bytes 1638416 | tf_op jit(solution)/shard_map/psum | solution.py:440
  253.4 2.7 copy.17
  256.1 121.4 %all-reduce.8.cloned.1.call-done = (f32[640,640]{0,1:T(8,128)}, f32[640,4096]{1,0:T(8,128)}) async-done(((f32[640,640]{0,1:T(8,128)}, f32[640,4096]{1,0:T(8,128)}), (f32[640,640]{0,1:T(8,128)}, f32[640,4096]{1,0:T(8,128)})) %all-reduce.8.cloned.1.call-update) | async-done | bytes 12124176 | tf_op jit(solution)/shard_map/psum | solution.py:438
  377.5 2.7 copy.16
  380.2 9.3 %copy.23 = f32[640,4096]{1,0:T(8,128)} copy(f32[640,4096]{1,0:T(8,128)} %get-tuple-element.41) | data formatting | bytes 20971520
  (1 shorter events, 0.0 us)
Async XLA Ops:
  7.2 246.2 %all-reduce.6.cloned.1.call-start = ((), (), s32[]{:S(2)}) async-start(), calls=%async_computation | async-start | bytes 3276800 | tf_op jit(solution)/shard_map/psum | solution.py:440
  137.6 50.7 %copy-start.2 = (bf16[16,32,640]{2,1,0:T(8,128)(2,1)S(1)}, bf16[16,32,640]{2,1,0:T(8,128)(2,1)}, u32[]{:S(2)}) copy-start(bf16[16,32,640]{2,1,0:T(8,128)(2,1)} %param.9) | copy-start | bytes 1966084
  188.3 2.0 copy-start.3
  188.3 2.0 copy-start.4
  190.3 187.2 %all-reduce.8.cloned.1.call-start = ((), (), s32[]{:S(2)}) async-start(), calls=%async_computation.1 | async-start | bytes 24248320 | tf_op jit(solution)/shard_map/psum | solution.py:438
  191.9 1.1 copy-start
  191.9 2.2 copy-start.5
  191.9 2.7 copy-start.1
Sparse Core Ops, SparseCore 0:
  190.4 62.9 all-reduce.5
  257.6 119.7 all-reduce.7

commit v2 on v1

--- a/solution.py
+++ b/solution.py
@@ -14,11 +14,12 @@
 TILE_B = 512
 CHUNK = 512
 F32 = jnp.float32
+MESH_ID = pl.DeviceIdType.MESH
 BF16 = jnp.bfloat16
 
 
 def frame_of(dev, idx, n_seq, t_loc):
-    return dev * t_loc + idx
+    return idx * n_seq + dev
 
 
 def fwd_kernel(n_utt, t_loc, n_upos, nt_ref, nk_ref, enc_ref, pred_ref, wenc_ref, wpred_ref, w_ref, lab_ref,
@@ -29,7 +30,7 @@
 
     def per_utt(b, base):
         n_t = nt_ref[b]
-        a_utt = act_e[pl.ds(pl.multiple_of(b * t_loc, SUB), t_loc), :]
+        a_utt = [act_e[pl.ds(i * n_utt + b, 1), :] for i in range(t_loc)]
 
         def per_k(k, base):
             row = pl.multiple_of(b * n_upos + k * SUB, SUB)
@@ -37,7 +38,7 @@
             lab_k = lab_ref[pl.ds(row, SUB), :]
             for i in range(t_loc):
                 dst = pl.ds(pl.multiple_of((base + i) * SUB, SUB), SUB)
-                hf[dst, :] = jnp.tanh(a_utt[i:i + 1, :] + c_k)
+                hf[dst, :] = jnp.tanh(a_utt[i] + c_k)
                 labr[dst, :] = lab_k
             return base + n_t
 
@@ -145,13 +146,13 @@
     skew = n_upos + 1
     barrier = pltpu.get_barrier_semaphore()
     for p in range(1, n_seq):
-        pl.semaphore_signal(barrier, inc=1, device_id={"seq": lax.rem(me + p, n_seq)}, device_id_type=pl.DeviceIdType.MESH)
+        pl.semaphore_signal(barrier, inc=1, device_id={"seq": lax.rem(me + p, n_seq)}, device_id_type=MESH_ID)
     pl.semaphore_wait(barrier, n_seq - 1)
     copies = []
     for p in range(1, n_seq):
         cp = pltpu.make_async_remote_copy(
             src_ref=stat_ref.at[pl.ds(1, 2)], dst_ref=gath.at[me], send_sem=send_sem.at[p], recv_sem=recv_sem.at[p],
-            device_id={"seq": lax.rem(me + p, n_seq)}, device_id_type=pl.DeviceIdType.MESH)
+            device_id={"seq": lax.rem(me + p, n_seq)}, device_id_type=MESH_ID)
         cp.start()
         copies.append(cp)
     gath[me] = stat_ref[1:3]
@@ -231,8 +232,8 @@
         q_ref[1, k * SUB:(k + 1) * SUB, :] = acc1
 
 
-def bwd_kernel(n_utt, t_loc, n_upos, nt_ref, nk_ref, w_ref, lab_ref, stat_ref, q_ref, h_hbm, z_hbm,
-               dw_ref, da_ref, dc_ref, rlse, rq0, rq1, labr, dsr, zs, dzb, hbuf, ht, dhs, da_acc, zsem, hsem):
+def bwd_kernel(n_utt, t_loc, n_upos, nt_ref, nk_ref, w_ref, lab_ref, stat_ref, q_ref, enc_ref, wenc_ref, h_hbm, z_hbm,
+               dw_ref, gwe_ref, ge_ref, dc_ref, da_s, rlse, rq0, rq1, labr, dsr, zs, dzb, hbuf, ht, dhs, da_acc, zsem, hsem):
     vocab = w_ref.shape[1]
     half = vocab // 2
     lane8 = lax.broadcasted_iota(jnp.int32, (SUB, LANES), 1)
@@ -346,10 +347,240 @@
 
         base = lax.fori_loop(0, jnp.where(n_t > 0, nk_ref[b], 0), k_out, base)
         for i in range(t_loc):
-            da_ref[pl.ds(b * t_loc + i, 1), :] = jnp.sum(da_acc[i], axis=0, keepdims=True)
+            da_s[pl.ds(i * n_utt + b, 1), :] = jnp.sum(da_acc[i], axis=0, keepdims=True)
         return base
 
     lax.fori_loop(0, n_utt, utt_out, 0)
+    da16 = da_s[...].astype(BF16)
+    ge_ref[...] = lax.dot_general(da16, wenc_ref[...], (((1,), (1,)), ((), ())), preferred_element_type=F32).astype(BF16)
+    gwe_ref[...] = lax.dot_general(enc_ref[...], da16, (((0,), (0,)), ((), ())), preferred_element_type=F32)
+
+
+def exchange_kernel(n_seq, src_ref, out_ref, buf, send_sem, recv_sem):
+    me = lax.axis_index("seq")
+    barrier = pltpu.get_barrier_semaphore()
+    for p in range(1, n_seq):
+        pl.semaphore_signal(barrier, inc=1, device_id={"seq": lax.rem(me + p, n_seq)}, device_id_type=MESH_ID)
+    pl.semaphore_wait(barrier, n_seq - 1)
+    copies = []
+    for p in range(1, n_seq):
+        peer = lax.rem(me + p, n_seq)
+        copies.append(pltpu.make_async_remote_copy(src_ref=src_ref.at[peer], dst_ref=buf.at[me], send_sem=send_sem.at[p],
+                                                   recv_sem=recv_sem.at[p], device_id={"seq": peer}, device_id_type=MESH_ID))
+        copies[-1].start()
+    buf[me] = src_ref[me]
+    for cp in copies:
+        cp.wait()
+    out_ref[...] = buf[...]
+
+
+def reduce_kernel(n_seq, n_y, piece, dw_ref, gwe_ref, dc_ref, pred_ref, ge_ref, sum_ref, dc16_ref, geo_ref,
+                  acc, d2d, rb1, rb2, dcd, dcs, dcr, d2d_ss, d2d_rs, rs1_ss, rs1_rs, rs2_ss, rs2_rs, ag1_ss, ag1_rs,
+                  ag2_ss, ag2_rs, fw_ss, fw_rs, dc_ss, dc_rs, ge_ss, ge_rs):
+    me = lax.axis_index("seq")
+    y = lax.axis_index("data")
+    core = lax.rem(me, 2)
+    x = me // 2
+    n = n_y
+    other = 1 - core
+    partner = {"seq": x * 2 + other}
+    blk = 16 * piece
+    joint, vocab = dw_ref.shape
+    n_l = vocab // LANES
+    n_e = gwe_ref.shape[1] // LANES
+
+    def at(q, c, g, p1):
+        return pl.ds((((q * 2 + c) * 4 + g) * n + p1) * piece, piece)
+
+    def half(q, c):
+        return pl.ds((q * 2 + c) * blk, blk)
+
+    def copy(src, dst, ss, rs, dev):
+        return pltpu.make_async_remote_copy(src_ref=src, dst_ref=dst, send_sem=ss, recv_sem=rs, device_id=dev, device_id_type=MESH_ID)
+
+    def mod(v):
+        return lax.rem(v + 2 * n, n)
+
+    barrier = pltpu.get_barrier_semaphore()
+    peers = [{"seq": lax.rem(me + p, n_seq)} for p in range(1, n_seq)] + [{"data": mod(y + 1)}, {"data": mod(y - 1)}]
+    for dev in peers:
+        pl.semaphore_signal(barrier, inc=1, device_id=dev, device_id_type=MESH_ID)
+    pl.semaphore_wait(barrier, len(peers))
+
+    sends = []
+
+    def go(cp):
+        cp.start()
+        sends.append(cp)
+        return cp
+
+    dc_d2d = go(copy(dc_ref.at[:, other], dcd, dc_ss.at[0], dc_rs.at[0], partner))
+    ge_copies = []
+    for p in range(1, n_seq):
+        peer = lax.rem(me + p, n_seq)
+        ge_copies.append(go(copy(ge_ref.at[peer], geo_ref.at[me], ge_ss.at[p], ge_rs.at[p], {"seq": peer})))
+    geo_ref[me] = ge_ref[me]
+
+    def build_dw(g8, _):
+        for l in range(n_l):
+            acc[g8 * n_l + l] = dw_ref[pl.ds(pl.multiple_of(g8 * SUB, SUB), SUB), l * LANES:(l + 1) * LANES]
+        return 0
+
+    rows_q = 2 * blk // n_l
+    n_g8 = joint // SUB
+    base_e = n_g8 * n_l
+
+    def build_e(g8, _):
+        for l in range(n_e):
+            acc[base_e + g8 * n_e + l] = gwe_ref[pl.ds(pl.multiple_of(g8 * SUB, SUB), SUB), l * LANES:(l + 1) * LANES]
+        return 0
+
+    d2ds = []
+
+    def send_d2d(q):
+        d2ds.append(go(copy(acc.at[half(q, other)], d2d.at[q], d2d_ss.at[q], d2d_rs.at[q], partner)))
+
+    for q in range(n - 1):
+        lax.fori_loop(q * rows_q, min((q + 1) * rows_q, n_g8), build_dw, 0)
+        if q == n - 2:
+            lax.fori_loop(0, n_g8, build_e, 0)
+        send_d2d(q)
+
+    dc_d2d.wait_recv()
+    for i in range(n):
+        dcs[i] = dc_ref[i, core] + dcd[i]
+    dc_x = []
+    for p in range(1, n):
+        px = mod(x + p)
+        dc_x.append(go(copy(dcs.at[px], dcr.at[p], dc_ss.at[p], dc_rs.at[p], {"seq": px * 2 + core})))
+
+    groups = []
+    for g in range(4):
+        part, sgn = g // 2, 1 - 2 * (g % 2)
+        xdev, ydev = {"seq": mod(x + sgn) * 2 + core}, {"data": mod(y + sgn)}
+        groups.append((g, sgn, x, y, xdev, ydev) if part == 0 else (g, sgn, y, x, ydev, xdev))
+
+    rs1 = {}
+
+    def send_rs1(g, sgn, r, dev, s, q):
+        rs1[g, s, q] = go(copy(acc.at[at(q, core, g, mod(r - sgn * (1 + s)))], rb1.at[g, s, q], rs1_ss.at[g, s, q], rs1_rs.at[g, s, q], dev))
+
+    def join_d2d(q):
+        d2ds[q].wait_recv()
+        start = (q * 2 + core) * blk
+
+        def add(i, _):
+            acc[pl.ds(start + i * SUB, SUB)] += d2d[q, pl.ds(i * SUB, SUB)]
+            return 0
+
+        lax.fori_loop(0, blk // SUB, add, 0)
+        for g, sgn, r, r2, dev, dev2 in groups:
+            send_rs1(g, sgn, r, dev, 0, q)
+
+    for q in range(n - 1):
+        join_d2d(q)
+
+    for cp in dc_x:
+        cp.wait_recv()
+    dc16 = (dcs[x] + dcr[1] + dcr[2] + dcr[3]).astype(BF16)
+    dc16_ref[me] = dc16
+    rows = dc16.shape[0]
+    dc_g = [go(copy(dc16_ref.at[me], dc16_ref.at[me], dc_ss.at[4], dc_rs.at[4], partner))]
+    for p in range(1, n):
+        dc_g.append(go(copy(dc16_ref.at[me], dc16_ref.at[me], dc_ss.at[4 + p], dc_rs.at[4 + p], {"seq": mod(x + p) * 2 + core})))
+    gwp = lax.dot_general(pred_ref[pl.ds(pl.multiple_of(me * rows, SUB), rows), :], dc16, (((0,), (0,)), ((), ())), preferred_element_type=F32)
+    gwe_ref_rows = n_g8
+    base_p = base_e + n_g8 * n_e
+    for g8 in range(gwe_ref_rows):
+        for l in range(n_e):
+            acc[base_p + g8 * n_e + l] = gwp[g8 * SUB:(g8 + 1) * SUB, l * LANES:(l + 1) * LANES]
+    n_pad = acc.shape[0] - base_p - n_g8 * n_e
+    if n_pad:
+        acc[pl.ds(base_p + n_g8 * n_e, n_pad)] = jnp.zeros((n_pad, SUB, LANES), F32)
+    send_d2d(n - 1)
+    join_d2d(n - 1)
+
+    for s in range(n - 1):
+        for q in range(n):
+            for g, sgn, r, r2, dev, dev2 in groups:
+                rs1[g, s, q].wait_recv()
+                acc[at(q, core, g, mod(r - sgn * (2 + s)))] += rb1[g, s, q]
+                if s < n - 2:
+                    send_rs1(g, sgn, r, dev, s + 1, q)
+    rs2 = {}
+
+    def send_rs2(g, sgn, r, r2, dev2, s):
+        rs2[g, s] = go(copy(acc.at[at(mod(r2 - sgn * (1 + s)), core, g, r)], rb2.at[g, s], rs2_ss.at[g, s], rs2_rs.at[g, s], dev2))
+
+    for g, sgn, r, r2, dev, dev2 in groups:
+        send_rs2(g, sgn, r, r2, dev2, 0)
+    for s in range(n - 1):
+        for g, sgn, r, r2, dev, dev2 in groups:
+            rs2[g, s].wait_recv()
+            acc[at(mod(r2 - sgn * (2 + s)), core, g, r)] += rb2[g, s]
+            if s < n - 2:
+                send_rs2(g, sgn, r, r2, dev2, s + 1)
+
+    ag1, ag2, fw = {}, {}, {}
+
+    def send_ag1(g, sgn, r, r2, dev2, s):
+        loc = at(mod(r2 - sgn * s), core, g, r)
+        ag1[g, s] = go(copy(sum_ref.at[loc], sum_ref.at[loc], ag1_ss.at[g, s], ag1_rs.at[g, s], dev2))
+
+    def send_ag2(g, sgn, r, r2, dev, s, k):
+        loc = at(mod(r2 - sgn * k), core, g, mod(r - sgn * s))
+        if s < n - 1:
+            ag2[g, s, k] = go(copy(sum_ref.at[loc], sum_ref.at[loc], ag2_ss.at[g, s, k], ag2_rs.at[g, s, k], dev))
+        fw[g, s, k] = go(copy(sum_ref.at[loc], sum_ref.at[loc], fw_ss.at[g, s, k], fw_rs.at[g, s, k], partner))
+
+    for g, sgn, r, r2, dev, dev2 in groups:
+        sum_ref[at(r2, core, g, r)] = acc[at(r2, core, g, r)]
+        send_ag1(g, sgn, r, r2, dev2, 0)
+        send_ag2(g, sgn, r, r2, dev, 0, 0)
+
+    def recv_ag1(s):
+        for g, sgn, r, r2, dev, dev2 in groups:
+            ag1[g, s].wait_recv()
+            if s < n - 2:
+                send_ag1(g, sgn, r, r2, dev2, s + 1)
+            send_ag2(g, sgn, r, r2, dev, 0, s + 1)
+
+    def recv_ag2(s, k):
+        for g, sgn, r, r2, dev, dev2 in groups:
+            ag2[g, s, k].wait_recv()
+            send_ag2(g, sgn, r, r2, dev, s + 1, k)
+
+    recv_ag1(0)
+    recv_ag1(1)
+    recv_ag2(0, 0)
+    recv_ag1(2)
+    for s in range(n - 1):
+        for k in range(n):
+            if (s, k) != (0, 0):
+                recv_ag2(s, k)
+    for cp in dc_g[1:]:
+        cp.wait_recv()
+    dc_f = []
+    for p in range(1, n):
+        blk_id = mod(x - p) * 2 + core
+        dc_f.append(go(copy(dc16_ref.at[blk_id], dc16_ref.at[blk_id], dc_ss.at[7 + p], dc_rs.at[7 + p], partner)))
+    dc_g[0].wait_recv()
+    for cp in dc_f:
+        cp.wait_recv()
+    for cp in ge_copies:
+        cp.wait_recv()
+    for key in fw:
+        fw[key].wait_recv()
+    for cp in sends:
+        cp.wait_send()
+
+
+def unpack_kernel(a_ref, b_ref, c_ref, wo_ref, we_ref, wp_ref):
+    for src, dst in ((a_ref, wo_ref), (b_ref, we_ref), (c_ref, wp_ref)):
+        n_l = dst.shape[1] // LANES
+        for g8 in range(dst.shape[0] // SUB):
+            for l in range(n_l):
+                dst[g8 * SUB:(g8 + 1) * SUB, l * LANES:(l + 1) * LANES] = src[g8 * n_l + l]
 
 
 VMEM = pl.BlockSpec(memory_space=pltpu.VMEM)
@@ -360,6 +591,7 @@
 
 def solution(mesh):
     n_seq = mesh.shape["seq"]
+    n_y = mesh.shape["data"]
     utt_rows = P(("part", "data"))
     utt_mats = P(("part", "data"), None)
     utt_cube = P(("part", "data"), None, None)
@@ -379,7 +611,15 @@
         lens = jnp.stack([jnp.tile(frame_len, LANES // n_utt), jnp.tile(label_len, LANES // n_utt)])
         cells = n_utt * t_loc * n_upos
         rows = cells + t_loc * SUB
-        enc2 = enc_loc.reshape(n_utt * t_loc, width)
+        enc_x = pl.pallas_call(
+            functools.partial(exchange_kernel, n_seq),
+            out_shape=jax.ShapeDtypeStruct((n_seq, n_utt, width), BF16),
+            in_specs=[VMEM], out_specs=VMEM,
+            scratch_shapes=[pltpu.VMEM((n_seq, n_utt, width), BF16), pltpu.SemaphoreType.DMA((n_seq,)), pltpu.SemaphoreType.DMA((n_seq,))],
+            compiler_params=pltpu.CompilerParams(collective_id=1, has_side_effects=True),
+            name="prep",
+        )(jnp.swapaxes(enc_loc, 0, 1))
+        enc2 = enc_x.reshape(n_utt * t_loc, width)
         pred2 = pred_loc.reshape(n_utt * n_upos, width)
 
         z, h, stat = pl.pallas_call(
@@ -412,13 +652,14 @@
             name="lattice",
         )(stat, lens)
 
-        dw_out, da, dc = pl.pallas_call(
+        dw_out, gwe, ge, dc = pl.pallas_call(
             functools.partial(bwd_kernel, n_utt, t_loc, n_upos),
-            out_shape=(jax.ShapeDtypeStruct((joint, vocab), F32), jax.ShapeDtypeStruct((n_utt * t_loc, joint), F32),
-                       jax.ShapeDtypeStruct((n_utt * n_upos, joint), F32)),
-            in_specs=[SMEM, SMEM] + [VMEM] * 4 + [HBM, HBM],
-            out_specs=(VMEM, VMEM, VMEM),
+            out_shape=(jax.ShapeDtypeStruct((joint, vocab), F32), jax.ShapeDtypeStruct((width, joint), F32),
+                       jax.ShapeDtypeStruct((n_utt * t_loc, width), BF16), jax.ShapeDtypeStruct((n_utt * n_upos, joint), F32)),
+            in_specs=[SMEM, SMEM] + [VMEM] * 6 + [HBM, HBM],
+            out_specs=(VMEM, VMEM, VMEM, VMEM),
             scratch_shapes=[
+                pltpu.VMEM((n_utt * t_loc, joint), F32),
                 pltpu.VMEM((rows, LANES), F32), pltpu.VMEM((rows, LANES), F32), pltpu.VMEM((rows, LANES), F32),
                 pltpu.VMEM((rows, LANES), jnp.int32), pltpu.VMEM((rows, joint), F32),
                 pltpu.VMEM((2, TILE_B, vocab // 2), F32), pltpu.VMEM((TILE_B, vocab), BF16), pltpu.VMEM((TILE_B, joint), BF16),
@@ -427,17 +668,46 @@
             ],
             compiler_params=pltpu.CompilerParams(vmem_limit_bytes=VMEM_LIMIT),
             name="joint_bwd",
-        )(n_live_t, n_live_k, w_out, lab_b, stat, occ, h, z)
-
-        da16 = da.astype(BF16)
-        grad_enc = jnp.einsum("rj,hj->rh", da16, w_enc, preferred_element_type=F32).astype(BF16).reshape(enc_loc.shape)
-        grad_w_enc = jnp.einsum("rh,rj->hj", enc2, da16, preferred_element_type=F32)
-        dc16 = lax.psum(dc, "seq").astype(BF16)
+        )(n_live_t, n_live_k, w_out, lab_b, stat, occ, enc2, w_enc, h, z)
+
+        n_x = n_seq // 2
+        assert n_x == n_y == 4 and t_loc == n_seq
+        tiles = joint * (vocab + 2 * width) // (SUB * LANES)
+        piece = pl.cdiv(tiles, 8 * n_x * n_y)
+        rows_s = n_utt * n_upos // n_seq
+        sem = pltpu.SemaphoreType.DMA
+        sums, dc16, ge_x = pl.pallas_call(
+            functools.partial(reduce_kernel, n_seq, n_y, piece),
+            out_shape=(jax.ShapeDtypeStruct((8 * n_x * n_y * piece, SUB, LANES), F32),
+                       jax.ShapeDtypeStruct((n_seq, rows_s, joint), BF16), jax.ShapeDtypeStruct((n_seq, n_utt, width), BF16)),
+            in_specs=[VMEM] * 5, out_specs=(VMEM, VMEM, VMEM),
+            scratch_shapes=[
+                pltpu.VMEM((8 * n_x * n_y * piece, SUB, LANES), F32), pltpu.VMEM((4, 16 * piece, SUB, LANES), F32),
+                pltpu.VMEM((4, 3, 4, piece, SUB, LANES), F32), pltpu.VMEM((4, 3, piece, SUB, LANES), F32),
+                pltpu.VMEM((n_x, rows_s, joint), F32), pltpu.VMEM((n_x, rows_s, joint), F32), pltpu.VMEM((n_x, rows_s, joint), F32),
+                sem((4,)), sem((4,)), sem((4, 3, 4)), sem((4, 3, 4)), sem((4, 3)), sem((4, 3)), sem((4, 3)), sem((4, 3)),
+                sem((4, 3, 4)), sem((4, 3, 4)), sem((4, 4, 4)), sem((4, 4, 4)), sem((11,)), sem((11,)), sem((n_seq,)), sem((n_seq,)),
+            ],
+            compiler_params=pltpu.CompilerParams(collective_id=2, has_side_effects=True, vmem_limit_bytes=VMEM_LIMIT),
+            name="reduce",
+        )(dw_out, gwe, dc.reshape(n_x, 2, rows_s, joint), pred2, ge.reshape(n_seq, n_utt, width))
+        grad_enc = jnp.swapaxes(ge_x, 0, 1)
+        dc16 = dc16.reshape(n_utt * n_upos, joint)
         grad_pred = jnp.einsum("rj,hj->rh", dc16, w_pred, preferred_element_type=F32).reshape(pred_loc.shape)
-        grad_w_pred = jnp.einsum("rh,rj->hj", pred2, dc16, preferred_element_type=F32)
-        grad_w_enc = lax.psum(grad_w_enc, ("data", "seq"))
-        grad_w_out = lax.psum(dw_out, ("data", "seq"))
-        grad_w_pred = lax.psum(grad_w_pred, "data")
+        steps = 10
+        row_b = joint // steps
+        n_o, n_e = row_b * vocab // (SUB * LANES), row_b * width // (SUB * LANES)
+        off_e, off_p = joint * vocab // (SUB * LANES) // n_e, joint * (vocab + width) // (SUB * LANES) // n_e
+        grad_w_out, grad_w_enc, grad_w_pred = pl.pallas_call(
+            unpack_kernel,
+            grid=(steps,),
+            out_shape=(jax.ShapeDtypeStruct((joint, vocab), F32), jax.ShapeDtypeStruct((width, joint), F32), jax.ShapeDtypeStruct((width, joint), F32)),
+            in_specs=[pl.BlockSpec((n_o, SUB, LANES), lambda i: (i, 0, 0)), pl.BlockSpec((n_e, SUB, LANES), lambda i: (off_e + i, 0, 0)),
+                      pl.BlockSpec((n_e, SUB, LANES), lambda i: (off_p + i, 0, 0))],
+            out_specs=(pl.BlockSpec((row_b, vocab), lambda i: (i, 0)), pl.BlockSpec((row_b, joint), lambda i: (i, 0)),
+                       pl.BlockSpec((row_b, joint), lambda i: (i, 0))),
+            name="unpack",
+        )(sums, sums, sums)
         return -logp[0, :n_utt], grad_enc, grad_pred, grad_w_enc, grad_w_pred, grad_w_out
 
     return jax.shard_map(body, mesh=mesh, in_specs=(enc_spec, utt_cube, weight_in, weight_in, weight_in, utt_mats, utt_rows, utt_rows), out_specs=(utt_rows, enc_spec, utt_cube, weight_out, weight_out, weight_out), check_vma=False)

time: 397 us -> 260 us (0.65)
  waiting for transfers between devices: 178 us -> 0 us
  Pallas kernels: 124 us -> 247 us
  blocking collectives: 50.7 us -> 0 us
  local copies, waits for them, and re-layouts: 19 us -> 5.02 us
  between operations: 14.2 us -> 0.73 us
    psum x2 -> x0, waiting for transfers between devices: 178 us -> none  [the longest x1 121 us: body(): grad_w_enc = lax.psum(grad_w_enc, ('data', 'seq'))]
    pallas_call x0 -> x3, Pallas kernels: none -> 153 us  [the longest x1 130 us: body(): pl.pallas_call(functools.partial(reduce_kernel, n_seq, n_y, piece), out_s...]
    psum x1 -> x0, blocking collectives: 50.7 us -> none  [body(): dc16 = lax.psum(dc, 'seq').astype(BF16)]
    pallas_call x1, Pallas kernels: 72.4 us -> 53.7 us  [body(): pl.pallas_call(functools.partial(bwd_kernel, n_utt, t_loc, n_upos), out_s...]
    unnamed x15 -> x8, local copies, waits for them, and re-layouts: 15.9 us -> 3.23 us
    pallas_call x1, Pallas kernels: 36.7 us -> 27.4 us  [body(): pl.pallas_call(functools.partial(fwd_kernel, n_utt, t_loc, n_upos), out_s...]
    dot_general x3 -> x0, matrix products: 4.47 us -> none  [the longest x1 1.87 us: body(): jnp.einsum('rh,rj->hj', pred2, dc16, preferred_element_type=F32)]
  transfers between devices with their start and end apart: 2 -> 0, of which waited for: 2 -> 0; matrix products, arithmetic and copies ran while one was open for 2% -> 0% of each run, Pallas kernels for 0% -> 0%
where the time goes in v2:
time: 260 us
  Pallas kernels  247 us (95%)
  local copies, waits for them, and re-layouts  5.02 us (2%)
  other arithmetic  4.3 us (2%)
  matrix products  2.93 us (1%)
    pallas_call x1, Pallas kernels, body(): pl.pallas_call(functools.partial(reduce_kernel, n_seq, n_y, piece), out_s...  130 us
    pallas_call x1, Pallas kernels, body(): pl.pallas_call(functools.partial(bwd_kernel, n_utt, t_loc, n_upos), out_s...  53.7 us
    pallas_call x1, Pallas kernels, body(): pl.pallas_call(functools.partial(fwd_kernel, n_utt, t_loc, n_upos), out_s...  27.4 us
    pallas_call x1, Pallas kernels, body(): pl.pallas_call(functools.partial(lattice_kernel, n_seq, t_loc, n_utt), ou...  13.2 us
    pallas_call x1, Pallas kernels, body(): pl.pallas_call(unpack_kernel, grid=(steps,), out_shape=(jax.ShapeDtypeStr...  12.7 us
    pallas_call x1, Pallas kernels, body(): pl.pallas_call(functools.partial(exchange_kernel, n_seq), out_shape=jax.S...  9.9 us

profile of v2, /device:TPU:97, one launch (start us, length us, event | category | flops | bytes accessed | tf_op | source)
XLA Modules:
  0.0 259.8 jit_solution(308149921517139132)
XLA Ops:
  0.6 0.0 copy-start.2
  0.6 0.0 copy-start.1
  0.7 1.4 convert_reduce_fusion.nt_ref
  2.0 1.2 fusion.2.nk_ref
  3.2 1.6 copy.19
  4.8 9.9 %prep.1 = bf16[8,16,640]{2,1,0:T(8,128)(2,1)} custom-call(bf16[8,16,640]{2,1,0:T(8,128)(2,1)} %bitcast.20), custom_call_target="tpu_custom_call" | custom-call | tf_op jit(solution)/shard_map/prep/pallas_call | solution.py:614
  14.7 0.7 concatenate.3
  15.4 0.1 broadcast_in_dim.4
  15.5 0.8 broadcast_in_dim.10.lab_ref
  16.4 27.4 %joint_fwd.1 = (f32[4096,4096]{1,0:T(8,128)}, bf16[4096,640]{1,0:T(8,128)(2,1)}, f32[3,32,128]{2,1,0:T(8,128)}) custom-call(s32[16]{0:T(128)} %convert_reduce_fusion.nt_ref, s32[16]{0:T(128)} %fusion.2.nk_ref, bf16[128,640]{1,0:T(8,128)(2,1)} %bitcast.17, bf16[512,640]{1,0:T(8,128)(2,1)} %bitcast.15, bf16[640,640]{1,0:T(8,128)(2,1)} %wenc_ref.3, ...), custom_call_target="tpu_custom_call" | custom-call | tf_op jit(solution)/shard_map/joint_fwd/pallas_call | solution.py:625
  43.7 0.0 copy-done.1
  43.8 0.1 stack_tile.7
  43.8 0.0 copy-done.2
  43.8 0.1 stack_tile.6
  43.9 0.6 pad_add_fusion.len_ref
  44.5 13.2 %lattice.1 = (f32[2,32,128]{2,1,0:T(8,128)}, f32[1,128]{1,0:T(1,128)}) custom-call(f32[3,32,128]{2,1,0:T(8,128)} %get-tuple-element.21.stat_ref, s32[2,128]{1,0:T(2,128)} %pad_add_fusion.len_ref), custom_call_target="tpu_custom_call" | custom-call | tf_op jit(solution)/shard_map/lattice/pallas_call | solution.py:644
  57.7 1.2 negate_bitcast_fusion
  58.8 53.7 %joint_bwd.1 = (f32[640,4096]{1,0:T(8,128)}, f32[640,640]{1,0:T(8,128)}, bf16[128,640]{1,0:T(8,128)(2,1)}, f32[512,640]{1,0:T(8,128)}) custom-call(s32[16]{0:T(128)} %convert_reduce_fusion.nt_ref, s32[16]{0:T(128)} %fusion.2.nk_ref, bf16[640,4096]{1,0:T(8,128)(2,1)} %w_ref.3, s32[512,128]{1,0:T(8,128)} %broadcast_in_dim.10.lab_ref, ...), custom_call_target="tpu_custom_call" | custom-call | tf_op jit(solution)/shard_map/joint_bwd/pallas_call | solution.py:655
  112.5 0.0 copy-start
  112.5 130.0 %reduce.1 = (f32[3456,8,128]{2,1,0:T(8,128)}, bf16[8,64,640]{2,1,0:T(8,128)(2,1)}, bf16[8,16,640]{2,1,0:T(8,128)(2,1)}) custom-call(f32[640,4096]{1,0:T(8,128)} %get-tuple-element.26.dw_ref, f32[640,640]{1,0:T(8,128)} %get-tuple-element.27.gwe_ref, f32[4,2,64,640]{3,2,1,0:T(8,128)} %bitcast.19, bf16[512,640]{1,0:T(8,128)(2,1)} %bitcast.16, ...), custom_call_target="tpu_custom_call" | custom-call | tf_op jit(solution)/shard_map/reduce/pallas_call | solution.py:679
  242.6 1.6 copy.17
  244.2 0.0 copy-done
  244.2 2.9 %fusion = f32[16,32,640]{2,1,0:T(8,128)} fusion(bf16[16,32,640]{2,1,0:T(8,128)(2,1)} %bitcast.21, bf16[640,640]{1,0:T(8,128)(2,1)S(1)} %copy-done), kind=kOutput, calls=%fused_computation | convolution fusion | flops 419430400 | bytes 2785280 | tf_op jit(solution)/shard_map/rj,hj->rh/dot_general | solution.py:696
  247.1 12.7 %unpack.1 = (f32[640,4096]{1,0:T(8,128)}, f32[640,640]{1,0:T(8,128)}, f32[640,640]{1,0:T(8,128)}) custom-call(f32[3456,8,128]{2,1,0:T(8,128)} %get-tuple-element.32.a_ref.b_ref.c_ref, f32[3456,8,128]{2,1,0:T(8,128)} %get-tuple-element.32.a_ref.b_ref.c_ref, f32[3456,8,128]{2,1,0:T(8,128)} %get-tuple-element.32.a_ref.b_ref.c_ref), custom_call_target="tpu_custom_call" | custom-call | tf_op jit(solution)/shard_map/unpack/pallas_call | solution.py:701
  (3 shorter events, 0.0 us)
Async XLA Ops:
  0.6 43.2 %copy-start.2 = (s32[16]{0:T(128)S(1)}, s32[16]{0:T(128)}, u32[]{:S(2)}) copy-start(s32[16]{0:T(128)} %param.14) | copy-start | bytes 196
  0.6 43.1 %copy-start.1 = (s32[16]{0:T(128)S(1)}, s32[16]{0:T(128)}, u32[]{:S(2)}) copy-start(s32[16]{0:T(128)} %param.15) | copy-start | bytes 196
  112.5 131.6 %copy-start = (bf16[640,640]{1,0:T(8,128)(2,1)S(1)}, bf16[640,640]{1,0:T(8,128)(2,1)}, u32[]{:S(2)}) copy-start(bf16[640,640]{1,0:T(8,128)(2,1)} %wpred_ref.1) | copy-start | bytes 2457604

commit v3 on v2

--- a/solution.py
+++ b/solution.py
@@ -22,9 +22,11 @@
     return idx * n_seq + dev
 
 
-def fwd_kernel(n_utt, t_loc, n_upos, nt_ref, nk_ref, enc_ref, pred_ref, wenc_ref, wpred_ref, w_ref, lab_ref,
-               z_hbm, h_hbm, stat_ref, act_e, act_p, hf, labr, rstat, zbuf, hbuf, m_s, s_s, l_s, zsem, hsem):
+def fwd_kernel(n_utt, t_loc, n_upos, nt_ref, nk_ref, enc_ref, pred_ref, wenc_ref, wpred_ref, w_hbm, lab_ref,
+               z_hbm, h_hbm, stat_ref, w_ref, wsem, act_e, act_p, hf, labr, rstat, zbuf, hbuf, m_s, s_s, l_s, zsem, hsem):
     vocab = w_ref.shape[1]
+    w_copy = pltpu.make_async_copy(w_hbm, w_ref, wsem)
+    w_copy.start()
     act_e[...] = jnp.dot(enc_ref[...], wenc_ref[...], preferred_element_type=F32).astype(BF16).astype(F32)
     act_p[...] = jnp.dot(pred_ref[...], wpred_ref[...], preferred_element_type=F32).astype(BF16).astype(F32)
 
@@ -54,6 +56,7 @@
         return 0
 
     lax.fori_loop(0, n_tiles * (TILE_F // SUB) - total, clear, 0)
+    w_copy.wait()
 
     def out_copies(n, slot):
         rows = pl.ds(pl.multiple_of(n * TILE_F, TILE_F), TILE_F)
@@ -232,10 +235,24 @@
         q_ref[1, k * SUB:(k + 1) * SUB, :] = acc1
 
 
-def bwd_kernel(n_utt, t_loc, n_upos, nt_ref, nk_ref, w_ref, lab_ref, stat_ref, q_ref, enc_ref, wenc_ref, h_hbm, z_hbm,
-               dw_ref, gwe_ref, ge_ref, dc_ref, da_s, rlse, rq0, rq1, labr, dsr, zs, dzb, hbuf, ht, dhs, da_acc, zsem, hsem):
+def bwd_kernel(n_utt, t_loc, n_upos, nt_ref, nk_ref, w_hbm, lab_ref, stat_ref, q_ref, enc_ref, wenc_ref, h_hbm, z_hbm,
+               dw_hbm, gwe_ref, ge_ref, dc_ref, w_ref, dw_ref, wsem, dwsem, da_s, rlse, rq0, rq1, labr, dsr, zs, dzb, hbuf, ht, dhs, da_acc, zsem, hsem):
     vocab = w_ref.shape[1]
     half = vocab // 2
+    w_copy = pltpu.make_async_copy(w_hbm, w_ref, wsem)
+
+    def in_copies(n, part):
+        rows = pl.ds(pl.multiple_of(n * TILE_B, TILE_B), TILE_B)
+        return pltpu.make_async_copy(z_hbm.at[rows, part * half:(part + 1) * half], zs.at[part], zsem.at[part])
+
+    def h_copy(n, slot):
+        return pltpu.make_async_copy(h_hbm.at[pl.ds(pl.multiple_of(n * TILE_B, TILE_B), TILE_B), :], hbuf.at[slot], hsem.at[slot])
+
+    h_copy(0, 0).start()
+    in_copies(0, 0).start()
+    w_copy.start()
+    in_copies(0, 1).start()
+
     lane8 = lax.broadcasted_iota(jnp.int32, (SUB, LANES), 1)
 
     def per_utt(b, base):
@@ -258,19 +275,6 @@
     total = lax.fori_loop(0, n_utt, per_utt, 0)
     n_tiles = pl.cdiv(total * SUB, TILE_B)
 
-    def in_copies(n, part):
-        rows = pl.ds(pl.multiple_of(n * TILE_B, TILE_B), TILE_B)
-        return pltpu.make_async_copy(z_hbm.at[rows, part * half:(part + 1) * half], zs.at[part], zsem.at[part])
-
-    def h_copy(n):
-        return pltpu.make_async_copy(h_hbm.at[pl.ds(pl.multiple_of(n * TILE_B, TILE_B), TILE_B), :], hbuf, hsem)
-
-    @pl.when(n_tiles > 0)
-    def _():
-        h_copy(0).start()
-        in_copies(0, 0).start()
-        in_copies(0, 1).start()
-
     def clear(r, _):
         dst = pl.ds(pl.multiple_of((total + r) * SUB, SUB), SUB)
         for ref in (rlse, rq0, rq1):
@@ -286,13 +290,16 @@
 
     lax.fori_loop(0, dw_ref.shape[0] // SUB, zero, 0)
     dc_ref[...] = jnp.zeros_like(dc_ref)
+    w_copy.wait()
 
     def tile(n, _):
         row0 = pl.multiple_of(n * TILE_B, TILE_B)
         nxt = jnp.minimum(n + 1, n_tiles - 1)
         lane = lax.broadcasted_iota(jnp.int32, (1, LANES), 1)
-        h_copy(n).wait()
-        ht[...] = jnp.transpose(hbuf[...])
+        slot = lax.rem(n, 2)
+        h_copy(n, slot).wait()
+        h_copy(nxt, 1 - slot).start()
+        ht[...] = jnp.transpose(hbuf[slot])
         grp = 16
         for part in range(2):
             in_copies(n, part).wait()
@@ -302,13 +309,14 @@
                     src = pl.ds(row0 + r, grp)
                     lse, q0, q1, lab = rlse[src, :], rq0[src, :], rq1[src, :], labr[src, :]
                     qs = q0 + q1
+                    off = lab - lane
                     for q in range(CHUNK // LANES):
                         loc = c * CHUNK + q * LANES
                         col = part * half + loc
                         dz = jnp.exp(zs[part, rs, loc:loc + LANES] - lse) * qs
                         if col == 0:
                             dz = dz - jnp.where(lane == 0, q0, 0.0)
-                        dz = dz - jnp.where(lab == lane + col, q1, 0.0)
+                        dz = dz - jnp.where(off == col, q1, 0.0)
                         dzb[rs, col:col + LANES] = dz.astype(BF16)
                 cs = slice(part * half + c * CHUNK, part * half + (c + 1) * CHUNK)
                 dw_ref[:, cs] += jnp.dot(ht[...], dzb[:, cs], preferred_element_type=F32)
@@ -318,18 +326,17 @@
             if part == 0:
                 dhs[...] = dh
             else:
-                h32 = hbuf[...].astype(F32)
+                h32 = hbuf[slot].astype(F32)
                 dsr[pl.ds(row0, TILE_B), :] = (dhs[...] + dh) * (1.0 - h32 * h32)
-        h_copy(nxt).start()
         return 0
 
     lax.fori_loop(0, n_tiles, tile, 0)
 
-    @pl.when(n_tiles > 0)
-    def _():
-        h_copy(n_tiles - 1).wait()
-        in_copies(n_tiles - 1, 0).wait()
-        in_copies(n_tiles - 1, 1).wait()
+    dw_copy = pltpu.make_async_copy(dw_ref, dw_hbm, dwsem)
+    dw_copy.start()
+    h_copy(n_tiles - 1, lax.rem(n_tiles, 2)).wait()
+    in_copies(n_tiles - 1, 0).wait()
+    in_copies(n_tiles - 1, 1).wait()
 
     def utt_out(b, base):
         n_t = nt_ref[b]
@@ -354,6 +361,7 @@
     da16 = da_s[...].astype(BF16)
     ge_ref[...] = lax.dot_general(da16, wenc_ref[...], (((1,), (1,)), ((), ())), preferred_element_type=F32).astype(BF16)
     gwe_ref[...] = lax.dot_general(enc_ref[...], da16, (((0,), (0,)), ((), ())), preferred_element_type=F32)
+    dw_copy.wait()
 
 
 def exchange_kernel(n_seq, src_ref, out_ref, buf, send_sem, recv_sem):
@@ -374,8 +382,8 @@
     out_ref[...] = buf[...]
 
 
-def reduce_kernel(n_seq, n_y, piece, dw_ref, gwe_ref, dc_ref, pred_ref, ge_ref, sum_ref, dc16_ref, geo_ref,
-                  acc, d2d, rb1, rb2, dcd, dcs, dcr, d2d_ss, d2d_rs, rs1_ss, rs1_rs, rs2_ss, rs2_rs, ag1_ss, ag1_rs,
+def reduce_kernel(n_seq, n_y, piece, dw_hbm, gwe_ref, dc_ref, pred_ref, ge_ref, sum_ref, dc16_ref, geo_ref,
+                  stg, st_sem, own_sem, acc, d2d, rb1, rb2, dcd, dcs, dcr, d2d_ss, d2d_rs, rs1_ss, rs1_rs, rs2_ss, rs2_rs, ag1_ss, ag1_rs,
                   ag2_ss, ag2_rs, fw_ss, fw_rs, dc_ss, dc_rs, ge_ss, ge_rs):
     me = lax.axis_index("seq")
     y = lax.axis_index("data")
@@ -385,7 +393,7 @@
     other = 1 - core
     partner = {"seq": x * 2 + other}
     blk = 16 * piece
-    joint, vocab = dw_ref.shape
+    joint, vocab = dw_hbm.shape
     n_l = vocab // LANES
     n_e = gwe_ref.shape[1] // LANES
 
@@ -421,14 +429,29 @@
         ge_copies.append(go(copy(ge_ref.at[peer], geo_ref.at[me], ge_ss.at[p], ge_rs.at[p], {"seq": peer})))
     geo_ref[me] = ge_ref[me]
 
-    def build_dw(g8, _):
-        for l in range(n_l):
-            acc[g8 * n_l + l] = dw_ref[pl.ds(pl.multiple_of(g8 * SUB, SUB), SUB), l * LANES:(l + 1) * LANES]
-        return 0
-
     rows_q = 2 * blk // n_l
     n_g8 = joint // SUB
     base_e = n_g8 * n_l
+    loads = []
+    for q in range(n - 1):
+        lo, hi = q * rows_q, min((q + 1) * rows_q, n_g8)
+        cp = pltpu.make_async_copy(dw_hbm.at[lo * SUB:hi * SUB, :], stg.at[q % 2, pl.ds(0, (hi - lo) * SUB), :], st_sem.at[q])
+        loads.append((cp, lo, hi))
+    loads[0][0].start()
+    loads[1][0].start()
+
+    def build_dw(q):
+        cp, lo, hi = loads[q]
+        cp.wait()
+
+        def row(g8, _):
+            for l in range(n_l):
+                acc[g8 * n_l + l] = stg[q % 2, pl.ds(pl.multiple_of((g8 - lo) * SUB, SUB), SUB), l * LANES:(l + 1) * LANES]
+            return 0
+
+        lax.fori_loop(lo, hi, row, 0)
+        if q + 2 < n - 1:
+            loads[q + 2][0].start()
 
     def build_e(g8, _):
         for l in range(n_e):
@@ -441,7 +464,7 @@
         d2ds.append(go(copy(acc.at[half(q, other)], d2d.at[q], d2d_ss.at[q], d2d_rs.at[q], partner)))
 
     for q in range(n - 1):
-        lax.fori_loop(q * rows_q, min((q + 1) * rows_q, n_g8), build_dw, 0)
+        build_dw(q)
         if q == n - 2:
             lax.fori_loop(0, n_g8, build_e, 0)
         send_d2d(q)
@@ -521,20 +544,23 @@
             if s < n - 2:
                 send_rs2(g, sgn, r, r2, dev2, s + 1)
 
-    ag1, ag2, fw = {}, {}, {}
+    ag1, ag2, fw, own = {}, {}, {}, []
 
     def send_ag1(g, sgn, r, r2, dev2, s):
         loc = at(mod(r2 - sgn * s), core, g, r)
-        ag1[g, s] = go(copy(sum_ref.at[loc], sum_ref.at[loc], ag1_ss.at[g, s], ag1_rs.at[g, s], dev2))
+        src = (sum_ref if s else acc).at[loc]
+        ag1[g, s] = go(copy(src, sum_ref.at[loc], ag1_ss.at[g, s], ag1_rs.at[g, s], dev2))
 
     def send_ag2(g, sgn, r, r2, dev, s, k):
         loc = at(mod(r2 - sgn * k), core, g, mod(r - sgn * s))
+        src = (sum_ref if s or k else acc).at[loc]
         if s < n - 1:
-            ag2[g, s, k] = go(copy(sum_ref.at[loc], sum_ref.at[loc], ag2_ss.at[g, s, k], ag2_rs.at[g, s, k], dev))
-        fw[g, s, k] = go(copy(sum_ref.at[loc], sum_ref.at[loc], fw_ss.at[g, s, k], fw_rs.at[g, s, k], partner))
+            ag2[g, s, k] = go(copy(src, sum_ref.at[loc], ag2_ss.at[g, s, k], ag2_rs.at[g, s, k], dev))
+        fw[g, s, k] = go(copy(src, sum_ref.at[loc], fw_ss.at[g, s, k], fw_rs.at[g, s, k], partner))
 
     for g, sgn, r, r2, dev, dev2 in groups:
-        sum_ref[at(r2, core, g, r)] = acc[at(r2, core, g, r)]
+        own.append(pltpu.make_async_copy(acc.at[at(r2, core, g, r)], sum_ref.at[at(r2, core, g, r)], own_sem.at[g]))
+        own[-1].start()
         send_ag1(g, sgn, r, r2, dev2, 0)
         send_ag2(g, sgn, r, r2, dev, 0, 0)
 
@@ -573,6 +599,8 @@
         fw[key].wait_recv()
     for cp in sends:
         cp.wait_send()
+    for cp in own:
+        cp.wait()
 
 
 def unpack_kernel(a_ref, b_ref, c_ref, wo_ref, we_ref, wp_ref):
@@ -587,6 +615,8 @@
 SMEM = pl.BlockSpec(memory_space=pltpu.SMEM)
 HBM = pl.BlockSpec(memory_space=pl.ANY)
 VMEM_LIMIT = 66_000_000
+REDUCE_VMEM = 46_000_000
+SUMS = HBM
 
 
 def solution(mesh):
@@ -626,9 +656,10 @@
             functools.partial(fwd_kernel, n_utt, t_loc, n_upos),
             out_shape=(jax.ShapeDtypeStruct((cells, vocab), F32), jax.ShapeDtypeStruct((cells, joint), BF16),
                        jax.ShapeDtypeStruct((3, n_upos, LANES), F32)),
-            in_specs=[SMEM, SMEM] + [VMEM] * 6,
+            in_specs=[SMEM, SMEM] + [VMEM] * 4 + [HBM, VMEM],
             out_specs=(HBM, HBM, VMEM),
             scratch_shapes=[
+                pltpu.VMEM((joint, vocab), BF16), pltpu.SemaphoreType.DMA,
                 pltpu.VMEM((n_utt * t_loc, joint), F32), pltpu.VMEM((n_utt * n_upos, joint), F32),
                 pltpu.VMEM((rows, joint), F32), pltpu.VMEM((rows, LANES), jnp.int32), pltpu.VMEM((3, rows, LANES), F32),
                 pltpu.VMEM((2, TILE_F, vocab), F32), pltpu.VMEM((2, TILE_F, joint), BF16),
@@ -656,15 +687,16 @@
             functools.partial(bwd_kernel, n_utt, t_loc, n_upos),
             out_shape=(jax.ShapeDtypeStruct((joint, vocab), F32), jax.ShapeDtypeStruct((width, joint), F32),
                        jax.ShapeDtypeStruct((n_utt * t_loc, width), BF16), jax.ShapeDtypeStruct((n_utt * n_upos, joint), F32)),
-            in_specs=[SMEM, SMEM] + [VMEM] * 6 + [HBM, HBM],
-            out_specs=(VMEM, VMEM, VMEM, VMEM),
+            in_specs=[SMEM, SMEM, HBM] + [VMEM] * 5 + [HBM, HBM],
+            out_specs=(HBM, VMEM, VMEM, VMEM),
             scratch_shapes=[
+                pltpu.VMEM((joint, vocab), BF16), pltpu.VMEM((joint, vocab), F32), pltpu.SemaphoreType.DMA, pltpu.SemaphoreType.DMA,
                 pltpu.VMEM((n_utt * t_loc, joint), F32),
                 pltpu.VMEM((rows, LANES), F32), pltpu.VMEM((rows, LANES), F32), pltpu.VMEM((rows, LANES), F32),
                 pltpu.VMEM((rows, LANES), jnp.int32), pltpu.VMEM((rows, joint), F32),
-                pltpu.VMEM((2, TILE_B, vocab // 2), F32), pltpu.VMEM((TILE_B, vocab), BF16), pltpu.VMEM((TILE_B, joint), BF16),
+                pltpu.VMEM((2, TILE_B, vocab // 2), F32), pltpu.VMEM((TILE_B, vocab), BF16), pltpu.VMEM((2, TILE_B, joint), BF16),
                 pltpu.VMEM((joint, TILE_B), BF16), pltpu.VMEM((TILE_B, joint), F32), pltpu.VMEM((t_loc, SUB, joint), F32),
-                pltpu.SemaphoreType.DMA((2,)), pltpu.SemaphoreType.DMA,
+                pltpu.SemaphoreType.DMA((2,)), pltpu.SemaphoreType.DMA((2,)),
             ],
             compiler_params=pltpu.CompilerParams(vmem_limit_bytes=VMEM_LIMIT),
             name="joint_bwd",
@@ -680,15 +712,16 @@
             functools.partial(reduce_kernel, n_seq, n_y, piece),
             out_shape=(jax.ShapeDtypeStruct((8 * n_x * n_y * piece, SUB, LANES), F32),
                        jax.ShapeDtypeStruct((n_seq, rows_s, joint), BF16), jax.ShapeDtypeStruct((n_seq, n_utt, width), BF16)),
-            in_specs=[VMEM] * 5, out_specs=(VMEM, VMEM, VMEM),
+            in_specs=[HBM] + [VMEM] * 4, out_specs=(SUMS, VMEM, VMEM),
             scratch_shapes=[
+                pltpu.VMEM((2, 2 * 16 * piece * SUB * LANES // vocab, vocab), F32), sem((3,)), sem((4,)),
                 pltpu.VMEM((8 * n_x * n_y * piece, SUB, LANES), F32), pltpu.VMEM((4, 16 * piece, SUB, LANES), F32),
                 pltpu.VMEM((4, 3, 4, piece, SUB, LANES), F32), pltpu.VMEM((4, 3, piece, SUB, LANES), F32),
                 pltpu.VMEM((n_x, rows_s, joint), F32), pltpu.VMEM((n_x, rows_s, joint), F32), pltpu.VMEM((n_x, rows_s, joint), F32),
                 sem((4,)), sem((4,)), sem((4, 3, 4)), sem((4, 3, 4)), sem((4, 3)), sem((4, 3)), sem((4, 3)), sem((4, 3)),
                 sem((4, 3, 4)), sem((4, 3, 4)), sem((4, 4, 4)), sem((4, 4, 4)), sem((11,)), sem((11,)), sem((n_seq,)), sem((n_seq,)),
             ],
-            compiler_params=pltpu.CompilerParams(collective_id=2, has_side_effects=True, vmem_limit_bytes=VMEM_LIMIT),
+            compiler_params=pltpu.CompilerParams(collective_id=2, has_side_effects=True, vmem_limit_bytes=REDUCE_VMEM),
             name="reduce",
         )(dw_out, gwe, dc.reshape(n_x, 2, rows_s, joint), pred2, ge.reshape(n_seq, n_utt, width))
         grad_enc = jnp.swapaxes(ge_x, 0, 1)
@@ -706,6 +739,7 @@
                       pl.BlockSpec((n_e, SUB, LANES), lambda i: (off_p + i, 0, 0))],
             out_specs=(pl.BlockSpec((row_b, vocab), lambda i: (i, 0)), pl.BlockSpec((row_b, joint), lambda i: (i, 0)),
                        pl.BlockSpec((row_b, joint), lambda i: (i, 0))),
+            compiler_params=pltpu.CompilerParams(vmem_limit_bytes=14_000_000),
             name="unpack",
         )(sums, sums, sums)
         return -logp[0, :n_utt], grad_enc, grad_pred, grad_w_enc, grad_w_pred, grad_w_out

time: 260 us -> 242 us (0.931)
  Pallas kernels: 247 us -> 221 us
  local copies, waits for them, and re-layouts: 5.02 us -> 12.8 us
    pallas_call x1, Pallas kernels: 130 us -> 121 us  [body(): pl.pallas_call(functools.partial(reduce_kernel, n_seq, n_y, piece), out_s...]
    pallas_call x1, Pallas kernels: 53.7 us -> 45.1 us  [body(): pl.pallas_call(functools.partial(bwd_kernel, n_utt, t_loc, n_upos), out_s...]
    unnamed x8 -> x18, local copies, waits for them, and re-layouts: 3.23 us -> 11 us
    pallas_call x1, Pallas kernels: 12.7 us -> 6.08 us  [body(): pl.pallas_call(unpack_kernel, grid=(steps,), out_shape=(jax.ShapeDtypeStr...]
where the time goes in v3:
time: 242 us; the launch traced here: 241 us
  Pallas kernels  221 us (91%)
  local copies, waits for them, and re-layouts  12.8 us (5%)
  other arithmetic  4.25 us (2%)
    pallas_call x1, Pallas kernels, body(): pl.pallas_call(functools.partial(reduce_kernel, n_seq, n_y, piece), out_s...  121 us
    pallas_call x1, Pallas kernels, body(): pl.pallas_call(functools.partial(bwd_kernel, n_utt, t_loc, n_upos), out_s...  45.1 us
    pallas_call x1, Pallas kernels, body(): pl.pallas_call(functools.partial(fwd_kernel, n_utt, t_loc, n_upos), out_s...  26.1 us
    pallas_call x1, Pallas kernels, body(): pl.pallas_call(functools.partial(lattice_kernel, n_seq, t_loc, n_utt), ou...  13.2 us
    unnamed x18, local copies, waits for them, and re-layouts  11 us
    pallas_call x1, Pallas kernels, body(): pl.pallas_call(functools.partial(exchange_kernel, n_seq), out_shape=jax.S...  9.91 us
    pallas_call x1, Pallas kernels, body(): pl.pallas_call(unpack_kernel, grid=(steps,), out_shape=(jax.ShapeDtypeStr...  6.08 us

profile of v3, /device:TPU:97, one launch (start us, length us, event | category | flops | bytes accessed | tf_op | source)
XLA Modules:
  0.0 240.9 jit_solution(11433951034679744729)
XLA Ops:
  0.6 0.0 copy-start.7
  0.6 0.0 copy-start.6
  0.7 1.3 convert_reduce_fusion.nt_ref
  1.9 1.2 fusion.2.nk_ref
  3.2 1.6 copy.19
  4.8 9.9 %prep.1 = bf16[8,16,640]{2,1,0:T(8,128)(2,1)} custom-call(bf16[8,16,640]{2,1,0:T(8,128)(2,1)} %bitcast.23), custom_call_target="tpu_custom_call" | custom-call | tf_op jit(solution)/shard_map/prep/pallas_call | solution.py:644
  14.7 0.7 concatenate.3
  15.4 0.1 broadcast_in_dim.4
  15.5 0.8 broadcast_in_dim.10.lab_ref
  16.3 26.1 %joint_fwd.1 = (f32[4096,4096]{1,0:T(8,128)}, bf16[4096,640]{1,0:T(8,128)(2,1)}, f32[3,32,128]{2,1,0:T(8,128)}) custom-call(s32[16]{0:T(128)} %convert_reduce_fusion.nt_ref, s32[16]{0:T(128)} %fusion.2.nk_ref, bf16[128,640]{1,0:T(8,128)(2,1)} %bitcast.21, bf16[512,640]{1,0:T(8,128)(2,1)} %bitcast.15, bf16[640,640]{1,0:T(8,128)(2,1)} %wenc_ref.3, ...), custom_call_target="tpu_custom_call" | custom-call | tf_op jit(solution)/shard_map/joint_fwd/pallas_call | solution.py:655
  42.4 0.0 copy-done.6
  42.4 0.1 stack_tile.7
  42.5 0.0 copy-done.7
  42.5 0.1 stack_tile.6
  42.6 0.6 pad_add_fusion.len_ref
  43.2 13.2 %lattice.1 = (f32[2,32,128]{2,1,0:T(8,128)}, f32[1,128]{1,0:T(1,128)}) custom-call(f32[3,32,128]{2,1,0:T(8,128)} %get-tuple-element.21.stat_ref, s32[2,128]{1,0:T(2,128)} %pad_add_fusion.len_ref), custom_call_target="tpu_custom_call" | custom-call | tf_op jit(solution)/shard_map/lattice/pallas_call | solution.py:675
  56.3 1.2 negate_bitcast_fusion
  57.5 0.0 copy-start.1
  57.5 45.1 %joint_bwd.1 = (f32[640,4096]{1,0:T(8,128)}, f32[640,640]{1,0:T(8,128)}, bf16[128,640]{1,0:T(8,128)(2,1)}, f32[512,640]{1,0:T(8,128)}) custom-call(s32[16]{0:T(128)} %convert_reduce_fusion.nt_ref, s32[16]{0:T(128)} %fusion.2.nk_ref, bf16[640,4096]{1,0:T(8,128)(2,1)} %w_hbm.3, s32[512,128]{1,0:T(8,128)} %broadcast_in_dim.10.lab_ref, ...), custom_call_target="tpu_custom_call" | custom-call | tf_op jit(solution)/shard_map/joint_bwd/pallas_call | solution.py:686
  102.6 0.0 copy-done.1
  102.7 0.0 copy-start.2
  102.7 1.4 copy-done.2
  104.1 0.0 copy-start.3
  104.1 1.3 copy-done.3
  105.4 0.0 copy-start.4
  105.4 0.9 copy-done.4
  106.3 0.0 copy-start.5
  106.3 120.9 %reduce.1 = (f32[3456,8,128]{2,1,0:T(8,128)}, bf16[8,64,640]{2,1,0:T(8,128)(2,1)S(1)}, bf16[8,16,640]{2,1,0:T(8,128)(2,1)S(1)}) custom-call(f32[640,4096]{1,0:T(8,128)} %get-tuple-element.26.dw_hbm, f32[640,640]{1,0:T(8,128)S(1)} %copy-done.2, f32[4,2,64,640]{3,2,1,0:T(8,128)S(1)} %bitcast.17, bf16[512,640]{1,0:T(8,128)(2,1)S(1)} %bitcast.16, ...), custom_call_target="tpu_custom_call" | custom-call | tf_op jit(solution)/shard_map/reduce/pallas_call | solution.py:711
  227.2 0.7 copy.17
  227.9 0.0 copy-done.5
  227.9 1.9 fusion
  229.8 0.0 copy-start
  229.8 5.0 %copy-done = f32[3456,8,128]{2,1,0:T(8,128)S(1)} copy-done((f32[3456,8,128]{2,1,0:T(8,128)S(1)}, f32[3456,8,128]{2,1,0:T(8,128)}, u32[]{:S(2)}) %copy-start) | copy-done | bytes 14155800
  234.8 6.1 %unpack.1 = (f32[640,4096]{1,0:T(8,128)}, f32[640,640]{1,0:T(8,128)}, f32[640,640]{1,0:T(8,128)}) custom-call(f32[3456,8,128]{2,1,0:T(8,128)S(1)} %copy-done, f32[3456,8,128]{2,1,0:T(8,128)S(1)} %copy-done, f32[3456,8,128]{2,1,0:T(8,128)S(1)} %copy-done), custom_call_target="tpu_custom_call" | custom-call | tf_op jit(solution)/shard_map/unpack/pallas_call | solution.py:734
  (3 shorter events, 0.0 us)
Async XLA Ops:
  0.6 41.9 %copy-start.7 = (s32[16]{0:T(128)S(1)}, s32[16]{0:T(128)}, u32[]{:S(2)}) copy-start(s32[16]{0:T(128)} %param.14) | copy-start | bytes 196
  0.6 41.8 %copy-start.6 = (s32[16]{0:T(128)S(1)}, s32[16]{0:T(128)}, u32[]{:S(2)}) copy-start(s32[16]{0:T(128)} %param.15) | copy-start | bytes 196
  57.5 45.1 %copy-start.1 = (bf16[16,32,640]{2,1,0:T(8,128)(2,1)S(1)}, bf16[16,32,640]{2,1,0:T(8,128)(2,1)}, u32[]{:S(2)}) copy-start(bf16[16,32,640]{2,1,0:T(8,128)(2,1)} %param.9) | copy-start | bytes 1966084
  102.7 1.4 copy-start.2
  104.1 1.3 copy-start.3
  105.4 0.9 copy-start.4
  106.3 121.6 %copy-start.5 = (bf16[640,640]{1,0:T(8,128)(2,1)S(1)}, bf16[640,640]{1,0:T(8,128)(2,1)}, u32[]{:S(2)}) copy-start(bf16[640,640]{1,0:T(8,128)(2,1)} %wpred_ref.1) | copy-start | bytes 2457604
  229.8 5.0 %copy-start = (f32[3456,8,128]{2,1,0:T(8,128)S(1)}, f32[3456,8,128]{2,1,0:T(8,128)}, u32[]{:S(2)}) copy-start(f32[3456,8,128]{2,1,0:T(8,128)} %get-tuple-element.32.a_ref.b_ref.c_ref) | copy-start | bytes 42467332

commit v4 on v3

--- a/solution.py
+++ b/solution.py
@@ -22,7 +22,12 @@
     return idx * n_seq + dev
 
 
-def fwd_kernel(n_utt, t_loc, n_upos, nt_ref, nk_ref, enc_ref, pred_ref, wenc_ref, wpred_ref, w_hbm, lab_ref,
+def live_chunks(b, n_seq, flen_ref, ulen_ref):
+    n_t = (flen_ref[b] - lax.axis_index("seq") + n_seq - 1) // n_seq
+    return n_t, jnp.where(n_t > 0, ulen_ref[b] // SUB + 1, 0)
+
+
+def fwd_kernel(n_utt, t_loc, n_upos, n_seq, flen_ref, ulen_ref, enc_ref, pred_ref, wenc_ref, wpred_ref, w_hbm, lab_ref,
                z_hbm, h_hbm, stat_ref, w_ref, wsem, act_e, act_p, hf, labr, rstat, zbuf, hbuf, m_s, s_s, l_s, zsem, hsem):
     vocab = w_ref.shape[1]
     w_copy = pltpu.make_async_copy(w_hbm, w_ref, wsem)
@@ -31,7 +36,7 @@
     act_p[...] = jnp.dot(pred_ref[...], wpred_ref[...], preferred_element_type=F32).astype(BF16).astype(F32)
 
     def per_utt(b, base):
-        n_t = nt_ref[b]
+        n_t, n_k = live_chunks(b, n_seq, flen_ref, ulen_ref)
         a_utt = [act_e[pl.ds(i * n_utt + b, 1), :] for i in range(t_loc)]
 
         def per_k(k, base):
@@ -44,10 +49,10 @@
                 labr[dst, :] = lab_k
             return base + n_t
 
-        return lax.fori_loop(0, jnp.where(n_t > 0, nk_ref[b], 0), per_k, base)
+        return lax.fori_loop(0, n_k, per_k, base)
 
     total = lax.fori_loop(0, n_utt, per_utt, 0)
-    n_tiles = pl.cdiv(total * SUB, TILE_B) * (TILE_B // TILE_F)
+    n_tiles = pl.cdiv(total * SUB, TILE_F)
 
     def clear(r, _):
         dst = pl.ds(pl.multiple_of((total + r) * SUB, SUB), SUB)
@@ -114,7 +119,7 @@
     lane8 = lax.broadcasted_iota(jnp.int32, (SUB, LANES), 1)
 
     def utt_out(b, base):
-        n_t = nt_ref[b]
+        n_t, n_k = live_chunks(b, n_seq, flen_ref, ulen_ref)
 
         def k_out(k, base):
             us = pl.ds(pl.multiple_of(k * SUB, SUB), SUB)
@@ -127,13 +132,13 @@
                 stat_ref[s, us, :] = acc[s]
             return base + n_t
 
-        return lax.fori_loop(0, jnp.where(n_t > 0, nk_ref[b], 0), k_out, base)
+        return lax.fori_loop(0, n_k, k_out, base)
 
     lax.fori_loop(0, n_utt, utt_out, 0)
 
-    @pl.when(n_tiles > 0)
-    def _():
-        for back in (2, 1):
+    for back in (2, 1):
+        @pl.when(n_tiles >= back)
+        def _():
             for cp in out_copies(n_tiles - back, lax.rem(n_tiles - back, 2)):
                 cp.wait()
 
@@ -142,7 +147,7 @@
     return jnp.maximum(x, y) + jnp.log(1.0 + jnp.exp(-jnp.abs(x - y)))
 
 
-def lattice_kernel(n_seq, t_loc, n_utt, stat_ref, len_ref, q_ref, logp_ref, gath, bsk, lsk, asv, xsv, ysv, send_sem, recv_sem):
+def lattice_kernel(n_seq, t_loc, n_utt, stat_ref, flen_ref, ulen_ref, q_ref, logp_ref, gath, bsk, lsk, asv, xsv, ysv, send_sem, recv_sem):
     me = lax.axis_index("seq")
     n_upos = stat_ref.shape[1]
     n_diag = bsk.shape[0] // n_upos
@@ -173,8 +178,12 @@
 
     upos = lax.broadcasted_iota(jnp.int32, (n_upos, LANES), 0)
     lane = lax.broadcasted_iota(jnp.int32, (n_upos, LANES), 1)
-    t_len = len_ref[0:1, :]
-    u_len = len_ref[1:2, :]
+    utt = lane[0:1] % n_utt
+    t_len = jnp.zeros((1, LANES), jnp.int32)
+    u_len = jnp.zeros((1, LANES), jnp.int32)
+    for b in range(n_utt):
+        t_len = jnp.where(utt == b, flen_ref[b], t_len)
+        u_len = jnp.where(utt == b, ulen_ref[b], u_len)
 
     def place(dev, _):
         t_lane = frame_of(dev, lane // n_utt, n_seq, t_loc)
@@ -213,7 +222,7 @@
         return log_add(x, y), jnp.where(end_diag == e, 0.0, log_add(xb, yb)), logp
 
     start = jnp.where(first, 0.0, fill)
-    _, _, logp = lax.fori_loop(0, n_diag, step, (start, fill, jnp.zeros_like(fill)))
+    _, _, logp = lax.fori_loop(0, n_diag, step, (start, fill, jnp.zeros_like(fill)), unroll=4)
     logp = jnp.sum(logp, axis=0, keepdims=True)
     logp_ref[...] = logp
     for k in range(n_upos // SUB):
@@ -235,7 +244,7 @@
         q_ref[1, k * SUB:(k + 1) * SUB, :] = acc1
 
 
-def bwd_kernel(n_utt, t_loc, n_upos, nt_ref, nk_ref, w_hbm, lab_ref, stat_ref, q_ref, enc_ref, wenc_ref, h_hbm, z_hbm,
+def bwd_kernel(n_utt, t_loc, n_upos, n_seq, flen_ref, ulen_ref, w_hbm, lab_ref, stat_ref, q_ref, enc_ref, wenc_ref, h_hbm, z_hbm,
                dw_hbm, gwe_ref, ge_ref, dc_ref, w_ref, dw_ref, wsem, dwsem, da_s, rlse, rq0, rq1, labr, dsr, zs, dzb, hbuf, ht, dhs, da_acc, zsem, hsem):
     vocab = w_ref.shape[1]
     half = vocab // 2
@@ -256,7 +265,7 @@
     lane8 = lax.broadcasted_iota(jnp.int32, (SUB, LANES), 1)
 
     def per_utt(b, base):
-        n_t = nt_ref[b]
+        n_t, n_k = live_chunks(b, n_seq, flen_ref, ulen_ref)
 
         def per_k(k, base):
             us = pl.ds(pl.multiple_of(k * SUB, SUB), SUB)
@@ -270,10 +279,12 @@
                 labr[dst, :] = lab_k
             return base + n_t
 
-        return lax.fori_loop(0, jnp.where(n_t > 0, nk_ref[b], 0), per_k, base)
+        return lax.fori_loop(0, n_k, per_k, base)
 
     total = lax.fori_loop(0, n_utt, per_utt, 0)
-    n_tiles = pl.cdiv(total * SUB, TILE_B)
+    n_half = pl.cdiv(total * SUB, TILE_F)
+    n_full = n_half // 2
+    n_tiles = pl.cdiv(n_half, 2)
 
     def clear(r, _):
         dst = pl.ds(pl.multiple_of((total + r) * SUB, SUB), SUB)
@@ -282,7 +293,7 @@
         labr[dst, :] = jnp.full((SUB, LANES), -1, jnp.int32)
         return 0
 
-    lax.fori_loop(0, n_tiles * (TILE_B // SUB) - total, clear, 0)
+    lax.fori_loop(0, n_half * (TILE_F // SUB) - total, clear, 0)
 
     def zero(r, _):
         dw_ref[pl.ds(pl.multiple_of(r * SUB, SUB), SUB), :] = jnp.zeros((SUB, vocab), F32)
@@ -292,19 +303,19 @@
     dc_ref[...] = jnp.zeros_like(dc_ref)
     w_copy.wait()
 
-    def tile(n, _):
+    def tile(n, size):
         row0 = pl.multiple_of(n * TILE_B, TILE_B)
         nxt = jnp.minimum(n + 1, n_tiles - 1)
         lane = lax.broadcasted_iota(jnp.int32, (1, LANES), 1)
         slot = lax.rem(n, 2)
         h_copy(n, slot).wait()
         h_copy(nxt, 1 - slot).start()
-        ht[...] = jnp.transpose(hbuf[slot])
+        ht[:, :size] = jnp.transpose(hbuf[slot, :size])
         grp = 16
         for part in range(2):
             in_copies(n, part).wait()
             for c in range(half // CHUNK):
-                for r in range(0, TILE_B, grp):
+                for r in range(0, size, grp):
                     rs = slice(r, r + grp)
                     src = pl.ds(row0 + r, grp)
                     lse, q0, q1, lab = rlse[src, :], rq0[src, :], rq1[src, :], labr[src, :]
@@ -319,27 +330,31 @@
                         dz = dz - jnp.where(off == col, q1, 0.0)
                         dzb[rs, col:col + LANES] = dz.astype(BF16)
                 cs = slice(part * half + c * CHUNK, part * half + (c + 1) * CHUNK)
-                dw_ref[:, cs] += jnp.dot(ht[...], dzb[:, cs], preferred_element_type=F32)
+                dw_ref[:, cs] += jnp.dot(ht[:, :size], dzb[:size, cs], preferred_element_type=F32)
             in_copies(nxt, part).start()
             cs = slice(part * half, (part + 1) * half)
-            dh = lax.dot_general(dzb[:, cs], w_ref[:, cs], (((1,), (1,)), ((), ())), preferred_element_type=F32)
+            dh = lax.dot_general(dzb[:size, cs], w_ref[:, cs], (((1,), (1,)), ((), ())), preferred_element_type=F32)
             if part == 0:
-                dhs[...] = dh
+                dhs[:size] = dh
             else:
-                h32 = hbuf[slot].astype(F32)
-                dsr[pl.ds(row0, TILE_B), :] = (dhs[...] + dh) * (1.0 - h32 * h32)
+                h32 = hbuf[slot, :size].astype(F32)
+                dsr[pl.ds(row0, size), :] = (dhs[:size] + dh) * (1.0 - h32 * h32)
+
+    def full(n, _):
+        tile(n, TILE_B)
         return 0
 
-    lax.fori_loop(0, n_tiles, tile, 0)
+    lax.fori_loop(0, n_full, full, 0)
+
+    @pl.when(n_full < n_tiles)
+    def _():
+        tile(n_full, TILE_F)
 
     dw_copy = pltpu.make_async_copy(dw_ref, dw_hbm, dwsem)
     dw_copy.start()
-    h_copy(n_tiles - 1, lax.rem(n_tiles, 2)).wait()
-    in_copies(n_tiles - 1, 0).wait()
-    in_copies(n_tiles - 1, 1).wait()
 
     def utt_out(b, base):
-        n_t = nt_ref[b]
+        n_t, n_k = live_chunks(b, n_seq, flen_ref, ulen_ref)
         da_acc[...] = jnp.zeros_like(da_acc)
 
         def k_out(k, base):
@@ -352,7 +367,7 @@
             dc_ref[pl.ds(pl.multiple_of(b * n_upos + k * SUB, SUB), SUB), :] = acc
             return base + n_t
 
-        base = lax.fori_loop(0, jnp.where(n_t > 0, nk_ref[b], 0), k_out, base)
+        base = lax.fori_loop(0, n_k, k_out, base)
         for i in range(t_loc):
             da_s[pl.ds(i * n_utt + b, 1), :] = jnp.sum(da_acc[i], axis=0, keepdims=True)
         return base
@@ -362,6 +377,9 @@
     ge_ref[...] = lax.dot_general(da16, wenc_ref[...], (((1,), (1,)), ((), ())), preferred_element_type=F32).astype(BF16)
     gwe_ref[...] = lax.dot_general(enc_ref[...], da16, (((0,), (0,)), ((), ())), preferred_element_type=F32)
     dw_copy.wait()
+    h_copy(n_tiles - 1, lax.rem(n_tiles, 2)).wait()
+    in_copies(n_tiles - 1, 0).wait()
+    in_copies(n_tiles - 1, 1).wait()
 
 
 def exchange_kernel(n_seq, src_ref, out_ref, buf, send_sem, recv_sem):
@@ -633,12 +651,8 @@
         n_utt, t_loc, width = enc_loc.shape
         n_upos = pred_loc.shape[1]
         joint, vocab = w_out.shape
-        me = lax.axis_index("seq")
         lab_ids = jnp.concatenate([labels, jnp.zeros((n_utt, 1), jnp.int32)], axis=1)
         lab_b = jnp.broadcast_to(lab_ids.reshape(n_utt * n_upos, 1), (n_utt * n_upos, LANES))
-        n_live_t = jnp.sum(frame_of(me, jnp.arange(t_loc), n_seq, t_loc)[None, :] < frame_len[:, None], axis=1, dtype=jnp.int32)
-        n_live_k = label_len // SUB + 1
-        lens = jnp.stack([jnp.tile(frame_len, LANES // n_utt), jnp.tile(label_len, LANES // n_utt)])
         cells = n_utt * t_loc * n_upos
         rows = cells + t_loc * SUB
         enc_x = pl.pallas_call(
@@ -653,7 +667,7 @@
         pred2 = pred_loc.reshape(n_utt * n_upos, width)
 
         z, h, stat = pl.pallas_call(
-            functools.partial(fwd_kernel, n_utt, t_loc, n_upos),
+            functools.partial(fwd_kernel, n_utt, t_loc, n_upos, n_seq),
             out_shape=(jax.ShapeDtypeStruct((cells, vocab), F32), jax.ShapeDtypeStruct((cells, joint), BF16),
                        jax.ShapeDtypeStruct((3, n_upos, LANES), F32)),
             in_specs=[SMEM, SMEM] + [VMEM] * 4 + [HBM, VMEM],
@@ -668,23 +682,23 @@
             ],
             compiler_params=pltpu.CompilerParams(vmem_limit_bytes=VMEM_LIMIT),
             name="joint_fwd",
-        )(n_live_t, n_live_k, enc2, pred2, w_enc, w_pred, w_out, lab_b)
+        )(frame_len, label_len, enc2, pred2, w_enc, w_pred, w_out, lab_b)
 
         n_diag = n_seq * t_loc + n_upos
         sk = pltpu.VMEM((n_diag * n_upos, LANES), F32)
         occ, logp = pl.pallas_call(
             functools.partial(lattice_kernel, n_seq, t_loc, n_utt),
             out_shape=(jax.ShapeDtypeStruct((2, n_upos, LANES), F32), jax.ShapeDtypeStruct((1, LANES), F32)),
-            in_specs=[VMEM, VMEM],
+            in_specs=[VMEM, SMEM, SMEM],
             out_specs=(VMEM, VMEM),
             scratch_shapes=[pltpu.VMEM((n_seq, 2, n_upos, LANES), F32), sk, sk, sk, sk, sk,
                             pltpu.SemaphoreType.DMA((n_seq,)), pltpu.SemaphoreType.DMA((n_seq,))],
             compiler_params=pltpu.CompilerParams(collective_id=0, has_side_effects=True, vmem_limit_bytes=VMEM_LIMIT),
             name="lattice",
-        )(stat, lens)
+        )(stat, frame_len, label_len)
 
         dw_out, gwe, ge, dc = pl.pallas_call(
-            functools.partial(bwd_kernel, n_utt, t_loc, n_upos),
+            functools.partial(bwd_kernel, n_utt, t_loc, n_upos, n_seq),
             out_shape=(jax.ShapeDtypeStruct((joint, vocab), F32), jax.ShapeDtypeStruct((width, joint), F32),
                        jax.ShapeDtypeStruct((n_utt * t_loc, width), BF16), jax.ShapeDtypeStruct((n_utt * n_upos, joint), F32)),
             in_specs=[SMEM, SMEM, HBM] + [VMEM] * 5 + [HBM, HBM],
@@ -700,7 +714,7 @@
             ],
             compiler_params=pltpu.CompilerParams(vmem_limit_bytes=VMEM_LIMIT),
             name="joint_bwd",
-        )(n_live_t, n_live_k, w_out, lab_b, stat, occ, enc2, w_enc, h, z)
+        )(frame_len, label_len, w_out, lab_b, stat, occ, enc2, w_enc, h, z)
 
         n_x = n_seq // 2
         assert n_x == n_y == 4 and t_loc == n_seq
@@ -710,7 +724,7 @@
         sem = pltpu.SemaphoreType.DMA
         sums, dc16, ge_x = pl.pallas_call(
             functools.partial(reduce_kernel, n_seq, n_y, piece),
-            out_shape=(jax.ShapeDtypeStruct((8 * n_x * n_y * piece, SUB, LANES), F32),
+            out_shape=(pltpu.VMEM((8 * n_x * n_y * piece, SUB, LANES), F32),
                        jax.ShapeDtypeStruct((n_seq, rows_s, joint), BF16), jax.ShapeDtypeStruct((n_seq, n_utt, width), BF16)),
             in_specs=[HBM] + [VMEM] * 4, out_specs=(SUMS, VMEM, VMEM),
             scratch_shapes=[

time: 242 us -> 230 us (0.950)
  local copies, waits for them, and re-layouts: 12.8 us -> 4.84 us
  other arithmetic: 4.25 us -> 1.17 us
  Pallas kernels: 221 us -> 218 us
    pallas_call x1, Pallas kernels: 121 us -> 111 us  [body(): pl.pallas_call(functools.partial(reduce_kernel, n_seq, n_y, piece), out_s...]
    pallas_call x2, Pallas kernels: 71.2 us -> 79.2 us  [the longest x1 50.4 us: body(): pl.pallas_call(functools.partial(bwd_kernel, n_utt, t_loc, n_upos, n_seq)...]
    unnamed x18 -> x4, local copies, waits for them, and re-layouts: 11 us -> 3.22 us
where the time goes in v4:
time: 230 us; the launch traced here: 228 us
  Pallas kernels  218 us (95%)
  local copies, waits for them, and re-layouts  4.84 us (2%)
  matrix products  2.92 us (1%)
    pallas_call x1, Pallas kernels, body(): pl.pallas_call(functools.partial(reduce_kernel, n_seq, n_y, piece), out_s...  111 us
    pallas_call x1, Pallas kernels, body(): pl.pallas_call(functools.partial(bwd_kernel, n_utt, t_loc, n_upos, n_seq)...  50.4 us
    pallas_call x1, Pallas kernels, body(): pl.pallas_call(functools.partial(fwd_kernel, n_utt, t_loc, n_upos, n_seq)...  28.8 us
    pallas_call x1, Pallas kernels, body(): pl.pallas_call(functools.partial(lattice_kernel, n_seq, t_loc, n_utt), ou...  12.5 us
    pallas_call x1, Pallas kernels, body(): pl.pallas_call(functools.partial(exchange_kernel, n_seq), out_shape=jax.S...  9.9 us
    pallas_call x1, Pallas kernels, body(): pl.pallas_call(unpack_kernel, grid=(steps,), out_shape=(jax.ShapeDtypeStr...  6.08 us

profile of v4, /device:TPU:97, one launch (start us, length us, event | category | flops | bytes accessed | tf_op | source)
XLA Modules:
  0.0 228.0 jit_solution(7118926394943125987)
XLA Ops:
  0.6 1.6 copy.17
  2.2 9.9 %prep.1 = bf16[8,16,640]{2,1,0:T(8,128)(2,1)} custom-call(bf16[8,16,640]{2,1,0:T(8,128)(2,1)} %bitcast.20), custom_call_target="tpu_custom_call" | custom-call | tf_op jit(solution)/shard_map/prep/pallas_call | solution.py:658
  12.1 0.7 concatenate.3
  12.8 0.1 broadcast_in_dim.7
  12.9 0.8 broadcast_in_dim.8.lab_ref
  13.8 28.8 %joint_fwd.1 = (f32[4096,4096]{1,0:T(8,128)}, bf16[4096,640]{1,0:T(8,128)(2,1)}, f32[3,32,128]{2,1,0:T(8,128)}) custom-call(s32[16]{0:T(128)} %flen_ref.5, s32[16]{0:T(128)} %ulen_ref.5, bf16[128,640]{1,0:T(8,128)(2,1)} %bitcast.17, bf16[512,640]{1,0:T(8,128)(2,1)} %bitcast.15, bf16[640,640]{1,0:T(8,128)(2,1)} %wenc_ref.3, bf16[640,640]{1,0:T(8,128)(2,1)} %wpred_ref.1, ...), custom_call_target="tpu_custom_call" | custom-call | tf_op jit(solution)/shard_map/joint_fwd/pallas_call | solution.py:669
  42.6 12.5 %lattice.1 = (f32[2,32,128]{2,1,0:T(8,128)}, f32[1,128]{1,0:T(1,128)}) custom-call(f32[3,32,128]{2,1,0:T(8,128)} %get-tuple-element.21.stat_ref, s32[16]{0:T(128)} %flen_ref.5, s32[16]{0:T(128)} %ulen_ref.5), custom_call_target="tpu_custom_call" | custom-call | tf_op jit(solution)/shard_map/lattice/pallas_call | solution.py:689
  55.1 1.2 negate_bitcast_fusion
  56.3 50.4 %joint_bwd.1 = (f32[640,4096]{1,0:T(8,128)}, f32[640,640]{1,0:T(8,128)}, bf16[128,640]{1,0:T(8,128)(2,1)}, f32[512,640]{1,0:T(8,128)}) custom-call(s32[16]{0:T(128)} %flen_ref.5, s32[16]{0:T(128)} %ulen_ref.5, bf16[640,4096]{1,0:T(8,128)(2,1)} %w_hbm.3, s32[512,128]{1,0:T(8,128)} %broadcast_in_dim.8.lab_ref, f32[3,32,128]{2,1,0:T(8,128)} %get-tuple-element.21.stat_ref, ...), custom_call_target="tpu_custom_call" | custom-call | tf_op jit(solution)/shard_map/joint_bwd/pallas_call | solution.py:700
  106.7 0.0 copy-start
  106.7 110.7 %reduce.1 = (f32[3456,8,128]{2,1,0:T(8,128)S(1)}, bf16[8,64,640]{2,1,0:T(8,128)(2,1)}, bf16[8,16,640]{2,1,0:T(8,128)(2,1)}) custom-call(f32[640,4096]{1,0:T(8,128)} %get-tuple-element.26.dw_hbm, f32[640,640]{1,0:T(8,128)} %get-tuple-element.27.gwe_ref, f32[4,2,64,640]{3,2,1,0:T(8,128)} %bitcast.19, bf16[512,640]{1,0:T(8,128)(2,1)} %bitcast.16, ...), custom_call_target="tpu_custom_call" | custom-call | tf_op jit(solution)/shard_map/reduce/pallas_call | solution.py:725
  217.4 1.6 copy.15
  219.0 0.0 copy-done
  219.0 2.9 %fusion = f32[16,32,640]{2,1,0:T(8,128)} fusion(bf16[16,32,640]{2,1,0:T(8,128)(2,1)} %bitcast.21, bf16[640,640]{1,0:T(8,128)(2,1)S(1)} %copy-done), kind=kOutput, calls=%fused_computation | convolution fusion | flops 419430400 | bytes 2785280 | tf_op jit(solution)/shard_map/rj,hj->rh/dot_general | solution.py:743
  221.9 6.1 %unpack.1 = (f32[640,4096]{1,0:T(8,128)}, f32[640,640]{1,0:T(8,128)}, f32[640,640]{1,0:T(8,128)}) custom-call(f32[3456,8,128]{2,1,0:T(8,128)S(1)} %get-tuple-element.32.a_ref.b_ref.c_ref, f32[3456,8,128]{2,1,0:T(8,128)S(1)} %get-tuple-element.32.a_ref.b_ref.c_ref, f32[3456,8,128]{2,1,0:T(8,128)S(1)} %get-tuple-element.32.a_ref.b_ref.c_ref), custom_call_target="tpu_custom_call" | custom-call | tf_op jit(solution)/shard_map/unpack/pallas_call | solution.py:748
Async XLA Ops:
  106.7 112.4 %copy-start = (bf16[640,640]{1,0:T(8,128)(2,1)S(1)}, bf16[640,640]{1,0:T(8,128)(2,1)}, u32[]{:S(2)}) copy-start(bf16[640,640]{1,0:T(8,128)(2,1)} %wpred_ref.1) | copy-start | bytes 2457604

commit v5 on v4

--- a/solution.py
+++ b/solution.py
@@ -222,7 +222,7 @@
         return log_add(x, y), jnp.where(end_diag == e, 0.0, log_add(xb, yb)), logp
 
     start = jnp.where(first, 0.0, fill)
-    _, _, logp = lax.fori_loop(0, n_diag, step, (start, fill, jnp.zeros_like(fill)), unroll=4)
+    _, _, logp = lax.fori_loop(0, n_diag, step, (start, fill, jnp.zeros_like(fill)), unroll=8)
     logp = jnp.sum(logp, axis=0, keepdims=True)
     logp_ref[...] = logp
     for k in range(n_upos // SUB):
@@ -741,7 +741,7 @@
         grad_enc = jnp.swapaxes(ge_x, 0, 1)
         dc16 = dc16.reshape(n_utt * n_upos, joint)
         grad_pred = jnp.einsum("rj,hj->rh", dc16, w_pred, preferred_element_type=F32).reshape(pred_loc.shape)
-        steps = 10
+        steps = 5
         row_b = joint // steps
         n_o, n_e = row_b * vocab // (SUB * LANES), row_b * width // (SUB * LANES)
         off_e, off_p = joint * vocab // (SUB * LANES) // n_e, joint * (vocab + width) // (SUB * LANES) // n_e

time: 230 us -> 232 us (level)
  Pallas kernels: 218 us -> 222 us
    pallas_call x1, Pallas kernels: 111 us -> 116 us  [body(): pl.pallas_call(functools.partial(reduce_kernel, n_seq, n_y, piece), out_s...]
where the time goes in v5:
time: 232 us
  Pallas kernels  222 us (96%)
  local copies, waits for them, and re-layouts  4.84 us (2%)
  matrix products  2.93 us (1%)
    pallas_call x1, Pallas kernels, body(): pl.pallas_call(functools.partial(reduce_kernel, n_seq, n_y, piece), out_s...  116 us
    pallas_call x1, Pallas kernels, body(): pl.pallas_call(functools.partial(bwd_kernel, n_utt, t_loc, n_upos, n_seq)...  50 us
    pallas_call x1, Pallas kernels, body(): pl.pallas_call(functools.partial(fwd_kernel, n_utt, t_loc, n_upos, n_seq)...  28.6 us
    pallas_call x1, Pallas kernels, body(): pl.pallas_call(functools.partial(lattice_kernel, n_seq, t_loc, n_utt), ou...  12.6 us
    pallas_call x1, Pallas kernels, body(): pl.pallas_call(functools.partial(exchange_kernel, n_seq), out_shape=jax.S...  9.9 us
    pallas_call x1, Pallas kernels, body(): pl.pallas_call(unpack_kernel, grid=(steps,), out_shape=(jax.ShapeDtypeStr...  5.09 us

profile of v5, /device:TPU:97, one launch (start us, length us, event | category | flops | bytes accessed | tf_op | source)
XLA Modules:
  0.0 231.7 jit_solution(15989228326352814492)
XLA Ops:
  0.6 1.6 copy.17
  2.2 9.9 %prep.1 = bf16[8,16,640]{2,1,0:T(8,128)(2,1)} custom-call(bf16[8,16,640]{2,1,0:T(8,128)(2,1)} %bitcast.20), custom_call_target="tpu_custom_call" | custom-call | tf_op jit(solution)/shard_map/prep/pallas_call | solution.py:658
  12.1 0.7 concatenate.3
  12.8 0.1 broadcast_in_dim.7
  12.9 0.8 broadcast_in_dim.8.lab_ref
  13.8 28.6 %joint_fwd.1 = (f32[4096,4096]{1,0:T(8,128)}, bf16[4096,640]{1,0:T(8,128)(2,1)}, f32[3,32,128]{2,1,0:T(8,128)}) custom-call(s32[16]{0:T(128)} %flen_ref.5, s32[16]{0:T(128)} %ulen_ref.5, bf16[128,640]{1,0:T(8,128)(2,1)} %bitcast.17, bf16[512,640]{1,0:T(8,128)(2,1)} %bitcast.15, bf16[640,640]{1,0:T(8,128)(2,1)} %wenc_ref.3, bf16[640,640]{1,0:T(8,128)(2,1)} %wpred_ref.1, ...), custom_call_target="tpu_custom_call" | custom-call | tf_op jit(solution)/shard_map/joint_fwd/pallas_call | solution.py:669
  42.4 12.6 %lattice.1 = (f32[2,32,128]{2,1,0:T(8,128)}, f32[1,128]{1,0:T(1,128)}) custom-call(f32[3,32,128]{2,1,0:T(8,128)} %get-tuple-element.21.stat_ref, s32[16]{0:T(128)} %flen_ref.5, s32[16]{0:T(128)} %ulen_ref.5), custom_call_target="tpu_custom_call" | custom-call | tf_op jit(solution)/shard_map/lattice/pallas_call | solution.py:689
  55.0 1.2 negate_bitcast_fusion
  56.2 50.0 %joint_bwd.1 = (f32[640,4096]{1,0:T(8,128)}, f32[640,640]{1,0:T(8,128)}, bf16[128,640]{1,0:T(8,128)(2,1)}, f32[512,640]{1,0:T(8,128)}) custom-call(s32[16]{0:T(128)} %flen_ref.5, s32[16]{0:T(128)} %ulen_ref.5, bf16[640,4096]{1,0:T(8,128)(2,1)} %w_hbm.3, s32[512,128]{1,0:T(8,128)} %broadcast_in_dim.8.lab_ref, f32[3,32,128]{2,1,0:T(8,128)} %get-tuple-element.21.stat_ref, ...), custom_call_target="tpu_custom_call" | custom-call | tf_op jit(solution)/shard_map/joint_bwd/pallas_call | solution.py:700
  106.2 0.0 copy-start
  106.2 115.9 %reduce.1 = (f32[3456,8,128]{2,1,0:T(8,128)S(1)}, bf16[8,64,640]{2,1,0:T(8,128)(2,1)}, bf16[8,16,640]{2,1,0:T(8,128)(2,1)}) custom-call(f32[640,4096]{1,0:T(8,128)} %get-tuple-element.26.dw_hbm, f32[640,640]{1,0:T(8,128)} %get-tuple-element.27.gwe_ref, f32[4,2,64,640]{3,2,1,0:T(8,128)} %bitcast.19, bf16[512,640]{1,0:T(8,128)(2,1)} %bitcast.16, ...), custom_call_target="tpu_custom_call" | custom-call | tf_op jit(solution)/shard_map/reduce/pallas_call | solution.py:725
  222.1 1.6 copy.15
  223.7 0.0 copy-done
  223.7 2.9 %fusion = f32[16,32,640]{2,1,0:T(8,128)} fusion(bf16[16,32,640]{2,1,0:T(8,128)(2,1)} %bitcast.21, bf16[640,640]{1,0:T(8,128)(2,1)S(1)} %copy-done), kind=kOutput, calls=%fused_computation | convolution fusion | flops 419430400 | bytes 2785280 | tf_op jit(solution)/shard_map/rj,hj->rh/dot_general | solution.py:743
  226.6 5.1 %unpack.1 = (f32[640,4096]{1,0:T(8,128)}, f32[640,640]{1,0:T(8,128)}, f32[640,640]{1,0:T(8,128)}) custom-call(f32[3456,8,128]{2,1,0:T(8,128)S(1)} %get-tuple-element.32.a_ref.b_ref.c_ref, f32[3456,8,128]{2,1,0:T(8,128)S(1)} %get-tuple-element.32.a_ref.b_ref.c_ref, f32[3456,8,128]{2,1,0:T(8,128)S(1)} %get-tuple-element.32.a_ref.b_ref.c_ref), custom_call_target="tpu_custom_call" | custom-call | tf_op jit(solution)/shard_map/unpack/pallas_call | solution.py:748
Async XLA Ops:
  106.2 117.6 %copy-start = (bf16[640,640]{1,0:T(8,128)(2,1)S(1)}, bf16[640,640]{1,0:T(8,128)(2,1)}, u32[]{:S(2)}) copy-start(bf16[640,640]{1,0:T(8,128)(2,1)} %wpred_ref.1) | copy-start | bytes 2457604
